TPU v7x, 32 devices: a whole 2x2x4 slice. The times are simulated.
32 devices in a mesh: tile: 16 (over z, y, core), shell: 2 (over x).
Axes of the slice: x: 2, y: 2, z: 4, core: 2. Of those that a mesh axis runs over, the one named last changes fastest.
Arguments:
- particles: bfloat16 [512, 2, 32768], P('tile', None, 'shell'), may hold values from -40 to 40
- projections: bfloat16 [512, 2, 32768], P('tile', None, 'shell'), may hold values from -6 to 6
- noise_weight: float32 [32768], P('shell'), may hold values from 0.001 to 0.012
- tile_list: int32 [512, 4], P('tile'), may hold values from 0 to 15, all different within a row; in each aligned block of 32 rows (0 to 31, 32 to 63, ...) at most 16 rows name the same one
- ori_start: int32 [512, 4], P('tile'), may hold values from 0 to 31
- shifts: int32 [512, 2], P('tile'), may hold values from -8 to 8
- defocus_bin: int32 [512], P('tile'), may hold values from 0 to 15
Outputs:
- posterior: float32 [512, 9, 64], P('tile')
- log_evidence: float32 [512], P('tile')
Inputs may be any that keep to these rules, and one draw needn't show every extreme that they name: `tile_list`: the 4 tiles of one particle differ, and among the particles of one index of tile no tile is named more than 16 times, a count reached.
All inputs are finite; a program needn't handle non-finite values.
Results may differ from a plain program's by a relative error of at most 0.0035.
Values may be sent and summed in bfloat16 or wider, within the bound.
A program may use at most 192 MiB of HBM per device.

v0:
```python
import functools
import math

import jax
import jax.numpy as jnp
from jax import lax
from jax.experimental import pallas as pl
from jax.experimental.pallas import tpu as pltpu
from jax.sharding import PartitionSpec as P

BOX = 256
NBIN = 16
TSIDE = 3


wave_length = 0.0197
aberration = 27000000.0
amplitude = 0.1
b_factor = 20.0
defocus_base = 5000.0
defocus_step = 500.0


def frequencies(first_index, span_count):
    flat_index = first_index + jnp.arange(span_count, dtype=jnp.int32)
    freq_x = flat_index // BOX
    freq_y = flat_index % BOX - BOX // 2
    return (freq_x, freq_y)


def ctf_table(freq_x, freq_y, bins_count):
    scaled_x = freq_x.astype(jnp.float32) / BOX
    scaled_y = freq_y.astype(jnp.float32) / BOX
    radius_sq = scaled_x * scaled_x + scaled_y * scaled_y
    defocus = defocus_base + defocus_step * jnp.arange(bins_count, dtype=jnp.float32)[:, None]
    aberr_phase = (
        math.pi * wave_length * defocus * radius_sq[None, :]
        - 0.5 * math.pi * aberration * wave_length**3 * radius_sq[None, :] ** 2
    )
    envelope = jnp.exp(-0.25 * b_factor * radius_sq)[None, :]
    return (
        -(math.sqrt(1.0 - amplitude**2) * jnp.sin(aberr_phase) + amplitude * jnp.cos(aberr_phase))
        * envelope
    )


def rotation(freq_x, freq_y, mult_x, mult_y):
    phase_turns = jnp.mod(freq_x * mult_x + freq_y * mult_y, BOX)
    angles = phase_turns.astype(jnp.float32) * (2.0 * math.pi / BOX)
    return (jnp.cos(angles), jnp.sin(angles))


def pick_rows(bin_index, lookup):
    one_hot = (bin_index[:, None] == jnp.arange(lookup.shape[0], dtype=jnp.int32)[None, :]).astype(
        jnp.float32
    )
    return jnp.dot(
        one_hot, lookup, precision=lax.Precision.HIGHEST, preferred_element_type=jnp.float32
    )


def prepare(particles, weight, ctf_rows, shifts, freq_x, freq_y):
    values = particles.astype(jnp.float32)
    real_part = values[:, 0]
    imag_part = values[:, 1]
    cosine, sine_value = rotation(freq_x[None, :], freq_y[None, :], shifts[:, 0:1], shifts[:, 1:2])
    moved_real = real_part * cosine + imag_part * sine_value
    moved_imag = imag_part * cosine - real_part * sine_value
    factor = weight[None, :] * ctf_rows
    weighted = jnp.stack([factor * moved_real, factor * moved_imag], axis=1).astype(jnp.bfloat16)
    energy = jnp.sum(weight[None, :] * (real_part * real_part + imag_part * imag_part), axis=1)
    return (weighted, energy)


def shifted_tables(projections, freq_x, freq_y):
    offsets = jnp.arange(TSIDE, dtype=jnp.int32) - TSIDE // 2
    mult_x = jnp.repeat(offsets, TSIDE)[:, None]
    mult_y = jnp.tile(offsets, TSIDE)[:, None]
    cosine, sine_value = rotation(freq_x[None, :], freq_y[None, :], mult_x, mult_y)
    cosine = cosine[:, None, :]
    sine_value = sine_value[:, None, :]
    proj_real = projections[:, 0].astype(jnp.float32)[None, :, :]
    proj_imag = projections[:, 1].astype(jnp.float32)[None, :, :]
    moved_real = proj_real * cosine - proj_imag * sine_value
    moved_imag = proj_imag * cosine + proj_real * sine_value
    stacked = jnp.stack([moved_real, moved_imag], axis=2).astype(jnp.bfloat16)
    return stacked.reshape(TSIDE * TSIDE * projections.shape[0], -1)


def slot_scores(slot_rows, bin_index, projections, weight, ctf, freq_x, freq_y):
    orient_count = projections.shape[0]
    lookup = shifted_tables(projections, freq_x, freq_y)
    cross_term = lax.dot_general(
        slot_rows, lookup, (((1,), (1,)), ((), ())), preferred_element_type=jnp.float32
    )
    cross_term = cross_term.reshape(slot_rows.shape[0], TSIDE * TSIDE, orient_count)
    proj_values = projections.astype(jnp.float32)
    magnitude = proj_values[:, 0] * proj_values[:, 0] + proj_values[:, 1] * proj_values[:, 1]
    weighted_ctf = weight[None, :] * ctf * ctf
    power = lax.dot_general(
        weighted_ctf,
        magnitude,
        (((1,), (1,)), ((), ())),
        precision=lax.Precision.HIGHEST,
        preferred_element_type=jnp.float32,
    )
    power_rows = pick_rows(bin_index, power)
    return cross_term - 0.5 * power_rows[:, None, :]


def window(scores, starts, orient_count):
    orient_index = jnp.mod(
        starts[:, None] + jnp.arange(orient_count // 2, dtype=jnp.int32)[None, :], orient_count
    )
    return jnp.take_along_axis(scores, orient_index[:, None, :], axis=2)


def slot_layout(tile_ids, tile_count, capacity):
    positions = jnp.arange(tile_ids.shape[0], dtype=jnp.int32)
    earlier_same = (tile_ids[:, None] == tile_ids[None, :]) & (
        positions[None, :] < positions[:, None]
    )
    slot_rank = jnp.sum(earlier_same.astype(jnp.int32), axis=1)
    slot_index = tile_ids * capacity + slot_rank
    matches = slot_index[None, :] == jnp.arange(tile_count * capacity, dtype=jnp.int32)[:, None]
    slot_owner = jnp.sum(jnp.where(matches, positions[None, :] + 1, 0), axis=1) - 1
    return (slot_index, slot_owner)


def finish(scores, energy_sum):
    scored = scores - 0.5 * energy_sum[:, None, None]
    row_peak = jnp.max(scored, axis=(1, 2))
    log_total = row_peak + jnp.log(jnp.sum(jnp.exp(scored - row_peak[:, None, None]), axis=(1, 2)))
    posterior = jnp.exp(scored - log_total[:, None, None])
    return (posterior, log_total)


def slot_plan(particles, projections, noise_weight, tile_list, ori_start, shifts, defocus_bin):
    tile_count = lax.axis_size("tile")
    band_index = lax.axis_index("shell")
    local_count = particles.shape[0]
    window_count = tile_list.shape[1]
    band_width = particles.shape[2]
    orient_count = projections.shape[0]
    capacity = max(2, (2 * local_count * window_count + tile_count - 1) // tile_count)
    freq_x, freq_y = frequencies(band_index * band_width, band_width)
    ctf = ctf_table(freq_x, freq_y, NBIN)
    weighted, energy = prepare(
        particles, noise_weight, pick_rows(defocus_bin, ctf), shifts, freq_x, freq_y
    )
    weighted = weighted.reshape(local_count, 2 * band_width)
    slot_index, slot_owner = slot_layout(tile_list.reshape(-1), tile_count, capacity)
    occupied = slot_owner >= 0
    item_index = jnp.maximum(slot_owner, 0)
    particle = item_index // window_count
    starts_flat = ori_start.reshape(-1)
    send_rows = jnp.where(
        occupied[:, None], jnp.take(weighted, particle, axis=0), jnp.zeros((), jnp.bfloat16)
    )
    send_rows = send_rows.reshape(tile_count, capacity, 2 * band_width)
    send_labels = jnp.stack(
        [jnp.take(defocus_bin, particle), jnp.take(starts_flat, item_index)], axis=1
    )
    send_labels = send_labels.astype(jnp.bfloat16).reshape(tile_count, capacity, 2)
    payload = lax.all_to_all(send_rows, "tile", split_axis=0, concat_axis=0, tiled=True)
    labels = lax.all_to_all(send_labels, "tile", split_axis=0, concat_axis=0, tiled=True)
    source_count = payload.shape[0]
    slot_count = payload.shape[1]
    slot_rows = payload.reshape(source_count * slot_count, payload.shape[2])
    label_ints = labels.reshape(source_count * slot_count, 2).astype(jnp.int32)
    partial_value = slot_scores(
        slot_rows, label_ints[:, 0], projections, noise_weight, ctf, freq_x, freq_y
    )
    partial_value = partial_value.reshape(
        source_count, slot_count, partial_value.shape[1], partial_value.shape[2]
    )
    returned = lax.all_to_all(partial_value, "tile", split_axis=0, concat_axis=0, tiled=True)
    candidates = returned.shape[2]
    returned = jnp.take(
        returned.reshape(tile_count * capacity, candidates, returned.shape[3]), slot_index, axis=0
    )
    returned = window(returned, starts_flat, orient_count)
    kept = returned.shape[2]
    returned = returned.reshape(local_count, window_count, candidates, kept)
    scores = jnp.transpose(returned, (0, 2, 1, 3)).reshape(
        local_count, candidates, window_count * kept
    )
    scores, energy_sum = lax.psum((scores, energy), "shell")
    return finish(scores, energy_sum)


SHIFT_MAX = 8
HIGH = lax.Precision.HIGHEST


def round_up(value, step):
    return (value + step - 1) // step * step


def weigh_kernel(part_ref, factor_ref, wave_y_ref, wave_x_ref, weight_ref, out_ref, energy_ref):
    rows, width = factor_ref.shape
    lines = width // BOX
    energy = jnp.zeros((rows, 1), jnp.float32)
    cos_y = wave_y_ref[:, :BOX]
    sin_y = wave_y_ref[:, BOX:]
    for line in range(lines):
        span = pl.ds(line * BOX, BOX)
        real_part = part_ref[0, 0, :, span].astype(jnp.float32)
        imag_part = part_ref[0, 1, :, span].astype(jnp.float32)
        cos_x = wave_x_ref[:, line : line + 1]
        sin_x = wave_x_ref[:, lines + line : lines + line + 1]
        cosine = cos_x * cos_y - sin_x * sin_y
        sine_value = sin_x * cos_y + cos_x * sin_y
        factor = factor_ref[:, span]
        out_ref[:, span] = (factor * (real_part * cosine + imag_part * sine_value)).astype(
            jnp.bfloat16
        )
        out_ref[:, pl.ds(width + line * BOX, BOX)] = (
            factor * (imag_part * cosine - real_part * sine_value)
        ).astype(jnp.bfloat16)
        square = real_part * real_part + imag_part * imag_part
        energy += jnp.sum(weight_ref[:, span] * square, axis=1, keepdims=True)
    energy_ref[...] = energy


def score_kernel(
    orients,
    proj_ref,
    power_ref,
    weighted_ref,
    energy_ref,
    hot_ref,
    tiles_ref,
    starts_ref,
    cos_ref,
    sin_ref,
    out_ref,
    moved_ref,
    chosen_ref,
    final_ref,
):
    step = pl.program_id(0)
    tiles = proj_ref.shape[0]
    width = proj_ref.shape[3]
    cands = TSIDE * TSIDE
    windows = tiles_ref.shape[0]
    block = cands * orients
    middle = cands // 2
    for tile in range(tiles):
        real_part = proj_ref[tile, 0].astype(jnp.float32)
        imag_part = proj_ref[tile, 1].astype(jnp.float32)

        def put(cand, real_value, imag_value):
            rows = pl.ds(tile * block + cand * orients, orients)
            moved_ref[rows, :width] = real_value.astype(jnp.bfloat16)
            moved_ref[rows, width:] = imag_value.astype(jnp.bfloat16)

        put(middle, real_part, imag_part)
        for cand in range(middle):
            cosine = cos_ref[cand : cand + 1, :]
            sine_value = sin_ref[cand : cand + 1, :]
            real_cos = real_part * cosine
            imag_sin = imag_part * sine_value
            imag_cos = imag_part * cosine
            real_sin = real_part * sine_value
            put(cand, real_cos - imag_sin, imag_cos + real_sin)
            put(cands - 1 - cand, real_cos + imag_sin, imag_cos - real_sin)
    cross = lax.dot_general(
        moved_ref[...],
        weighted_ref[...],
        (((1,), (1,)), ((), ())),
        preferred_element_type=jnp.float32,
    )
    power = jnp.dot(
        power_ref[...], hot_ref[...], precision=HIGH, preferred_element_type=jnp.float32
    )
    for tile in range(tiles):
        half_power = 0.5 * power[tile * orients : (tile + 1) * orients]
        named = [tiles_ref[j : j + 1, :] == step * tiles + tile for j in range(windows)]
        for cand in range(cands):
            first = tile * block + cand * orients
            value = cross[first : first + orients] - half_power
            rows = pl.ds(cand * orients, orients)
            for j in range(windows):
                chosen_ref[j, rows, :] = jnp.where(named[j], value, chosen_ref[j, rows, :])

    @pl.when(step == pl.num_programs(0) - 1)
    def _():
        kept = orients // 2
        used = cands * windows * kept
        for j in range(windows):
            start = starts_ref[j : j + 1, :]
            for cand in range(cands):
                value = chosen_ref[j, pl.ds(cand * orients, orients), :]
                bit = orients // 2
                while bit:
                    turned = pltpu.roll(value, orients - bit, 0)
                    value = jnp.where((start & bit) != 0, turned, value)
                    bit //= 2
                final_ref[pl.ds((cand * windows + j) * kept, kept), :] = value[:kept]
        spare = final_ref.shape[0] - used
        final_ref[pl.ds(used, spare), :] = jnp.zeros((spare, final_ref.shape[1]), jnp.float32)
        turned = final_ref[...].T
        column = lax.broadcasted_iota(jnp.int32, turned.shape, 1)
        out_ref[...] = jnp.where(column >= used, energy_ref[...], turned)


def split_band(values, tile_count):
    rows, pair, band_width = values.shape
    blocks = values.reshape(rows, pair, tile_count, band_width // tile_count)
    return jnp.transpose(blocks, (2, 1, 0, 3))


def exchange(blocks):
    return lax.all_to_all(blocks, "tile", split_axis=0, concat_axis=0, tiled=True)


def band_plan(particles, projections, noise_weight, tile_list, ori_start, shifts, defocus_bin):
    tile_count = lax.axis_size("tile")
    tile_index = lax.axis_index("tile")
    band_index = lax.axis_index("shell")
    local_count, pair, band_width = particles.shape
    orients = projections.shape[0]
    windows = tile_list.shape[1]
    width = band_width // tile_count
    lines = width // BOX
    count = local_count * tile_count
    cands = TSIDE * TSIDE

    labels = jnp.concatenate([tile_list, ori_start, shifts, defocus_bin[:, None]], axis=1).T
    labels = lax.all_gather(labels, "tile", axis=1, tiled=True)
    part_blocks, labels = lax.optimization_barrier((split_band(particles, tile_count), labels))
    part_in = exchange(part_blocks)
    proj_blocks, part_in = lax.optimization_barrier((split_band(projections, tile_count), part_in))
    proj_in = exchange(proj_blocks)

    tiles_all = labels[:windows]
    starts_all = labels[windows : 2 * windows]
    shift_x = labels[2 * windows]
    shift_y = labels[2 * windows + 1]
    bins = labels[2 * windows + 2]

    freq_x, freq_y = frequencies(band_index * band_width + tile_index * width, width)
    weight = lax.dynamic_slice_in_dim(noise_weight, tile_index * width, width, 0)
    ctf = ctf_table(freq_x, freq_y, NBIN)
    factor = pick_rows(bins, weight[None, :] * ctf)
    steps = jnp.arange(2 * SHIFT_MAX + 1, dtype=jnp.int32) - SHIFT_MAX
    none = jnp.zeros((), jnp.int32)
    own_y = jnp.arange(BOX, dtype=jnp.int32) - BOX // 2
    own_x = freq_x[::BOX]
    table_y = jnp.concatenate(rotation(own_y[None, :], own_y[None, :], none, steps[:, None]), axis=1)
    table_x = jnp.concatenate(rotation(own_x[None, :], own_x[None, :], steps[:, None], none), axis=1)
    wave_y = pick_rows(shift_y + SHIFT_MAX, table_y)
    wave_x = pick_rows(shift_x + SHIFT_MAX, table_x)

    weighted, energy = pl.pallas_call(
        weigh_kernel,
        grid=(tile_count,),
        in_specs=[
            pl.BlockSpec((1, pair, local_count, width), lambda i: (i, 0, 0, 0)),
            pl.BlockSpec((local_count, width), lambda i: (i, 0)),
            pl.BlockSpec((local_count, 2 * BOX), lambda i: (i, 0)),
            pl.BlockSpec((local_count, 2 * lines), lambda i: (i, 0)),
            pl.BlockSpec((1, width), lambda i: (0, 0)),
        ],
        out_specs=[
            pl.BlockSpec((local_count, pair * width), lambda i: (i, 0)),
            pl.BlockSpec((local_count, 1), lambda i: (i, 0)),
        ],
        out_shape=[
            jax.ShapeDtypeStruct((count, pair * width), jnp.bfloat16),
            jax.ShapeDtypeStruct((count, 1), jnp.float32),
        ],
        name="weigh",
    )(part_in, factor, wave_y, wave_x, weight[None, :])

    values = proj_in.astype(jnp.float32)
    magnitude = values[:, 0] * values[:, 0] + values[:, 1] * values[:, 1]
    power = lax.dot_general(
        magnitude.reshape(tile_count * orients, width),
        weight[None, :] * ctf * ctf,
        (((1,), (1,)), ((), ())),
        precision=HIGH,
        preferred_element_type=jnp.float32,
    )
    hot = (jnp.arange(NBIN, dtype=jnp.int32)[:, None] == bins[None, :]).astype(jnp.float32)
    offsets = jnp.arange(TSIDE, dtype=jnp.int32) - TSIDE // 2
    cos_t, sin_t = rotation(
        freq_x[None, :],
        freq_y[None, :],
        jnp.repeat(offsets, TSIDE)[:, None],
        jnp.tile(offsets, TSIDE)[:, None],
    )
    group = 2 if tile_count % 2 == 0 else 1
    used = cands * windows * (orients // 2)
    columns = round_up(used + 1, 128)

    def whole(*shape):
        return pl.BlockSpec(shape, lambda i: (0,) * len(shape))

    partial_value = pl.pallas_call(
        functools.partial(score_kernel, orients),
        grid=(tile_count // group,),
        in_specs=[
            pl.BlockSpec((group, pair, orients, width), lambda i: (i, 0, 0, 0)),
            pl.BlockSpec((group * orients, NBIN), lambda i: (i, 0)),
            whole(count, pair * width),
            whole(count, 1),
            whole(NBIN, count),
            whole(windows, count),
            whole(windows, count),
            whole(cands, width),
            whole(cands, width),
        ],
        out_specs=whole(count, columns),
        out_shape=jax.ShapeDtypeStruct((count, columns), jnp.float32),
        scratch_shapes=[
            pltpu.VMEM((group * cands * orients, pair * width), jnp.bfloat16),
            pltpu.VMEM((windows, cands * orients, count), jnp.float32),
            pltpu.VMEM((columns, count), jnp.float32),
        ],
        compiler_params=pltpu.CompilerParams(vmem_limit_bytes=48 * 1024 * 1024),
        name="score",
    )(proj_in, power, weighted, energy, hot, tiles_all, starts_all, cos_t, sin_t)

    blocks = partial_value.reshape(tile_count, local_count, columns)
    blocks = lax.all_to_all(blocks, "tile", split_axis=0, concat_axis=0, tiled=True)
    summed = jnp.sum(blocks, axis=0)
    summed = jnp.sum(lax.all_gather(summed, "shell", axis=0), axis=0)
    scores = summed[:, :used].reshape(local_count, cands, windows * (orients // 2))
    return finish(scores, summed[:, used])


def per_device(particles, projections, noise_weight, tile_list, ori_start, shifts, defocus_bin):
    piece = BOX * lax.axis_size("tile")
    plan = band_plan if particles.shape[2] % piece == 0 else slot_plan
    return plan(
        particles, projections, noise_weight, tile_list, ori_start, shifts, defocus_bin
    )


def solution(mesh):
    in_specs = (
        P("tile", None, "shell"),
        P("tile", None, "shell"),
        P("shell"),
        P("tile", None),
        P("tile", None),
        P("tile", None),
        P("tile"),
    )
    out_specs = (P("tile", None, None), P("tile"))
    return jax.shard_map(
        per_device, mesh=mesh, in_specs=in_specs, out_specs=out_specs, check_vma=False
    )
```

profile of v0, /device:TPU:0, one launch (start us, length us, event | category | flops | bytes accessed | tf_op | source)
XLA Modules:
  0.0 200.7 jit_solution(10302939723997716042)
XLA Ops:
  0.6 3.3 %reshape.138 = bf16[32,2,16,1024]{3,2,1,0:T(8,128)(2,1)S(1)} reshape(bf16[32,2,16384]{2,1,0:T(2,128)(2,1)} %param.7) | data formatting | bytes 4194304 | tf_op jit(solution)/shard_map/reshape | solution.py:310
  3.9 0.0 copy-start.5
  3.9 0.0 copy-start.6
  4.0 0.0 copy-start.7
  4.0 0.0 copy-start.8
  4.0 2.5 %copy.54 = bf16[32,2,16,1024]{3,0,1,2:T(8,128)(2,1)} copy(bf16[32,2,16,1024]{3,2,1,0:T(8,128)(2,1)S(1)} %reshape.138) | data formatting | bytes 4194304 | tf_op jit(solution)/shard_map/reshape | solution.py:310
  6.4 0.0 copy-done.5
  6.4 0.0 copy-done.6
  6.4 0.0 copy-done.7
  6.4 0.0 copy-done.8
  6.5 23.5 %all-gather.1 = s32[16,32,11]{1,2,0:T(8,128)S(1)} all-gather(s32[1,32,11]{1,2,0:T(8,128)S(1)} %add_bitcast_fusion), channel_id=1, replica_groups=mesh['tile'=16,'shell'=2] {'tile'}, dimensions={0}, use_global_device_ids=true | all-gather | bytes 23936 | tf_op jit(solution)/shard_map/all_gather | solution.py:331
  30.0 0.1 reshape.136
  30.1 3.7 %all-to-all-start = ((bf16[16,2,32,1024]{3,2,1,0:T(8,128)(2,1)}), bf16[16,2,32,1024]{3,2,1,0:T(8,128)(2,1)S(1)}, u32[]{:S(2)}, u32[]{:S(2)}) async-start(bf16[16,2,32,1024]{3,2,1,0:T(8,128)(2,1)} %bitcast.23), calls=%async_computation | async-start | bytes 4194304 | tf_op jit(solution)/shard_map/all_to_all | solution.py:315
  33.8 4.5 %reshape.137 = bf16[32,2,16,1024]{3,2,1,0:T(8,128)(2,1)} reshape(bf16[32,2,16384]{2,1,0:T(2,128)(2,1)} %param.8) | data formatting | bytes 4194304 | tf_op jit(solution)/shard_map/reshape | solution.py:310
  38.3 4.1 %copy.55 = bf16[32,2,16,1024]{3,0,1,2:T(8,128)(2,1)} copy(bf16[32,2,16,1024]{3,2,1,0:T(8,128)(2,1)} %reshape.137) | data formatting | bytes 4194304 | tf_op jit(solution)/shard_map/reshape | solution.py:310
  42.4 32.4 %all-to-all-done.part_ref = bf16[16,2,32,1024]{3,2,1,0:T(8,128)(2,1)S(1)} async-done(((bf16[16,2,32,1024]{3,2,1,0:T(8,128)(2,1)}), bf16[16,2,32,1024]{3,2,1,0:T(8,128)(2,1)S(1)}, u32[]{:S(2)}, u32[]{:S(2)}) %all-to-all-start) | async-done | bytes 2097184 | tf_op jit(solution)/shard_map/all_to_all | solution.py:315
  74.7 0.0 copy-start.2
  74.7 1.3 copy-done.2
  76.0 11.2 %all-to-all-start.1 = ((bf16[16,2,32,1024]{3,2,1,0:T(8,128)(2,1)}), bf16[16,2,32,1024]{3,2,1,0:T(8,128)(2,1)S(1)}, u32[]{:S(2)}, u32[]{:S(2)}) async-start(bf16[16,2,32,1024]{3,2,1,0:T(8,128)(2,1)} %bitcast.22), calls=%async_computation.1 | async-start | bytes 4194304 | tf_op jit(solution)/shard_map/all_to_all | solution.py:315
  87.3 0.1 slice.37
  87.4 0.1 mul.263
  87.5 0.1 broadcast_in_dim.8
  87.5 0.1 mul.259
  87.6 0.7 dynamic_slice.3
  88.3 0.0 copy-start.3
  88.4 0.1 fusion.51
  88.5 0.2 fusion.37
  88.7 0.3 fusion.15
  89.1 1.0 fusion.3.wave_x_ref
  90.1 1.7 fusion.2.wave_y_ref
  91.8 2.6 %fusion.1.factor_ref = f32[512,1024]{1,0:T(8,128)} fusion(s32[512]{0:T(512)S(1)} %bitcast.29, f32[1024]{0:T(1024)S(1)} %get-tuple-element.37, f32[1024]{0:T(1024)S(1)} %get-tuple-element.38, f32[1024]{0:T(1024)S(1)} %multiply_add_fusion, f32[16]{0:T(128)S(1)} %add_multiply_fusion, f32[1024]{0:T(1024)S(1)} %dynamic_slice.3), kind=kOutput, calls=%fused_computation.9 | convolution fusion | flops 100802560 | bytes 2115648 | tf_op jit(solution)/shard_map/dot_general | solution.py:57
  94.4 0.0 copy-done.3
  94.4 11.4 %weigh.1 = (bf16[512,2048]{1,0:T(8,128)(2,1)}, f32[512,1]{1,0:T(8,128)}) custom-call(bf16[16,2,32,1024]{3,2,1,0:T(8,128)(2,1)} %copy-done.2, f32[512,1024]{1,0:T(8,128)} %fusion.1.factor_ref, f32[512,512]{1,0:T(8,128)} %fusion.2.wave_y_ref, f32[512,8]{1,0:T(8,128)} %fusion.3.wave_x_ref, f32[1,1024]{1,0:T(1,128)} %bitcast.27), custom_call_target="tpu_custom_call" | custom-call | tf_op jit(solution)/shard_map/weigh/pallas_call | solution.py:356
  105.8 22.4 %all-to-all-done.1.proj_ref = bf16[16,2,32,1024]{3,2,1,0:T(8,128)(2,1)S(1)} async-done(((bf16[16,2,32,1024]{3,2,1,0:T(8,128)(2,1)}), bf16[16,2,32,1024]{3,2,1,0:T(8,128)(2,1)S(1)}, u32[]{:S(2)}, u32[]{:S(2)}) %all-to-all-start.1) | async-done | bytes 2097184 | tf_op jit(solution)/shard_map/all_to_all | solution.py:315
  128.2 0.5 convert_element_type.46
  128.7 0.0 copy-start.4
  128.7 0.6 fusion
  129.3 0.0 copy-start
  129.4 0.0 copy-start.1
  129.4 0.0 copy-done.4
  129.4 2.0 fusion.8.power_ref
  131.4 0.0 copy-done
  131.4 0.0 copy-done.1
  131.4 19.3 %score.1 = f32[512,640]{1,0:T(8,128)S(1)} custom-call(bf16[16,2,32,1024]{3,2,1,0:T(8,128)(2,1)S(1)} %all-to-all-done.1.proj_ref, f32[512,16]{1,0:T(8,128)S(1)} %fusion.8.power_ref, bf16[512,2048]{1,0:T(8,128)(2,1)S(1)} %copy-done, f32[512,1]{1,0:T(8,128)S(1)} %copy-done.1, f32[16,512]{1,0:T(8,128)S(1)} %fusion.31.hot_ref, ...), custom_call_target="tpu_custom_call" | custom-call | tf_op jit(solution)/shard_map/score/pallas_call | solution.py:401
  150.7 42.4 %all_to_all.15 = f32[16,32,640]{2,1,0:T(8,128)S(1)} all-to-all(f32[16,32,640]{2,1,0:T(8,128)S(1)} %bitcast.20), channel_id=1, replica_groups=mesh['tile'=16,'shell'=2] {'tile'}, dimensions={0} | all-to-all | bytes 2621440 | tf_op jit(solution)/shard_map/all_to_all | solution.py:427
  193.1 0.1 reduce_sum.27
  193.1 5.9 %all-gather = f32[64,640]{1,0:T(8,128)S(1)} all-gather(f32[32,640]{1,0:T(8,128)S(1)} %reduce_sum.27), channel_id=2, replica_groups=mesh['tile'=16,'shell'=2] {'shell'}, dimensions={0}, use_global_device_ids=true | all-gather | bytes 245760 | tf_op jit(solution)/shard_map/all_gather | solution.py:429
  199.1 0.2 fusion.35
  199.3 0.2 subtract_reduce_fusion
  199.5 0.2 exponential_reduce_fusion
  199.7 0.1 reshape.133
  199.8 0.0 copy-start.9
  199.8 0.1 subtract_exponential_fusion
  199.9 0.7 copy.45
  200.7 0.0 copy-done.9
  (15 shorter events, 0.2 us)
Async XLA Ops:
  3.9 2.5 %copy-start.5 = (s32[32,4]{0,1:T(4,128)S(1)}, s32[32,4]{0,1:T(4,128)}, u32[]{:S(2)}) copy-start(s32[32,4]{0,1:T(4,128)} %param.11) | copy-start | bytes 1540
  3.9 2.5 %copy-start.6 = (s32[32,4]{0,1:T(4,128)S(1)}, s32[32,4]{0,1:T(4,128)}, u32[]{:S(2)}) copy-start(s32[32,4]{0,1:T(4,128)} %param.10) | copy-start | bytes 1540
  4.0 2.5 %copy-start.7 = (s32[32,2]{0,1:T(2,128)S(1)}, s32[32,2]{0,1:T(2,128)}, u32[]{:S(2)}) copy-start(s32[32,2]{0,1:T(2,128)} %param.12) | copy-start | bytes 772
  4.0 2.5 %copy-start.8 = (s32[32]{0:T(128)S(1)}, s32[32]{0:T(128)}, u32[]{:S(2)}) copy-start(s32[32]{0:T(128)} %param.13) | copy-start | bytes 388
  30.1 44.7 %all-to-all-start = ((bf16[16,2,32,1024]{3,2,1,0:T(8,128)(2,1)}), bf16[16,2,32,1024]{3,2,1,0:T(8,128)(2,1)S(1)}, u32[]{:S(2)}, u32[]{:S(2)}) async-start(bf16[16,2,32,1024]{3,2,1,0:T(8,128)(2,1)} %bitcast.23), calls=%async_computation | async-start | bytes 4194304 | tf_op jit(solution)/shard_map/all_to_all | solution.py:315
  74.7 1.3 copy-start.2
  76.0 52.2 %all-to-all-start.1 = ((bf16[16,2,32,1024]{3,2,1,0:T(8,128)(2,1)}), bf16[16,2,32,1024]{3,2,1,0:T(8,128)(2,1)S(1)}, u32[]{:S(2)}, u32[]{:S(2)}) async-start(bf16[16,2,32,1024]{3,2,1,0:T(8,128)(2,1)} %bitcast.22), calls=%async_computation.1 | async-start | bytes 4194304 | tf_op jit(solution)/shard_map/all_to_all | solution.py:315
  88.3 6.1 %copy-start.3 = (f32[1024]{0:T(1024)}, f32[1024]{0:T(1024)S(1)}, u32[]{:S(2)}) copy-start(f32[1024]{0:T(1024)S(1)} %dynamic_slice.3) | copy-start | bytes 12292
  128.7 0.7 copy-start.4
  129.3 2.0 %copy-start = (bf16[512,2048]{1,0:T(8,128)(2,1)S(1)}, bf16[512,2048]{1,0:T(8,128)(2,1)}, u32[]{:S(2)}) copy-start(bf16[512,2048]{1,0:T(8,128)(2,1)} %get-tuple-element.12.weighted_ref) | copy-start | bytes 6291460
  129.4 2.0 %copy-start.1 = (f32[512,1]{1,0:T(8,128)S(1)}, f32[512,1]{1,0:T(8,128)}, u32[]{:S(2)}) copy-start(f32[512,1]{1,0:T(8,128)} %get-tuple-element.13.energy_ref) | copy-start | bytes 6148
  199.8 0.9 copy-start.9
where the time goes:
time: 201 us
  blocking collectives  71.8 us (36%)
  waiting for transfers between devices  54.8 us (27%)
  Pallas kernels  30.7 us (15%)
  local copies, waits for them, and re-layouts  17.7 us (9%)
  starting transfers between devices  14.9 us (7%)
  matrix products  7.3 us (4%)
  other arithmetic  2.64 us (1%)
    all_to_all x2, waiting for transfers between devices, exchange(): lax.all_to_all(blocks, 'tile', split_axis=0, concat_axis=0, tiled=True)  54.8 us
    all_to_all x1, blocking collectives, band_plan(): lax.all_to_all(blocks, 'tile', split_axis=0, concat_axis=0, tiled=True)  42.4 us
    all_gather x1, blocking collectives, band_plan(): labels = lax.all_gather(labels, 'tile', axis=1, tiled=True)  23.5 us
    pallas_call x1, Pallas kernels, band_plan(): pl.pallas_call(functools.partial(score_kernel, orients), grid=(tile_count...  19.3 us
    all_to_all x2, starting transfers between devices, exchange(): lax.all_to_all(blocks, 'tile', split_axis=0, concat_axis=0, tiled=True)  14.9 us
    reshape x4, local copies, waits for them, and re-layouts, split_band(): blocks = values.reshape(rows, pair, tile_count, band_width // tile_count)  14.3 us
    pallas_call x1, Pallas kernels, band_plan(): pl.pallas_call(weigh_kernel, grid=(tile_count,), in_specs=[pl.BlockSpec((...  11.4 us
    all_gather x1, blocking collectives, band_plan(): summed = jnp.sum(lax.all_gather(summed, 'shell', axis=0), axis=0)  5.94 us
  transfers between devices with their start and end apart: 2, of which 2 were waited for; matrix products, arithmetic and copies ran while one was open for 8% of the time, Pallas kernels for 6%

commit v1 on v0

v1 whole, which is shorter than its diff:
```python
import functools
import math

import jax
import jax.numpy as jnp
from jax import lax
from jax.experimental import pallas as pl
from jax.experimental.pallas import tpu as pltpu
from jax.sharding import PartitionSpec as P

BOX = 256
NBIN = 16
TSIDE = 3


wave_length = 0.0197
aberration = 27000000.0
amplitude = 0.1
b_factor = 20.0
defocus_base = 5000.0
defocus_step = 500.0


def frequencies(first_index, span_count):
    flat_index = first_index + jnp.arange(span_count, dtype=jnp.int32)
    freq_x = flat_index // BOX
    freq_y = flat_index % BOX - BOX // 2
    return (freq_x, freq_y)


def ctf_table(freq_x, freq_y, bins_count):
    scaled_x = freq_x.astype(jnp.float32) / BOX
    scaled_y = freq_y.astype(jnp.float32) / BOX
    radius_sq = scaled_x * scaled_x + scaled_y * scaled_y
    defocus = defocus_base + defocus_step * jnp.arange(bins_count, dtype=jnp.float32)[:, None]
    aberr_phase = (
        math.pi * wave_length * defocus * radius_sq[None, :]
        - 0.5 * math.pi * aberration * wave_length**3 * radius_sq[None, :] ** 2
    )
    envelope = jnp.exp(-0.25 * b_factor * radius_sq)[None, :]
    return (
        -(math.sqrt(1.0 - amplitude**2) * jnp.sin(aberr_phase) + amplitude * jnp.cos(aberr_phase))
        * envelope
    )


def rotation(freq_x, freq_y, mult_x, mult_y):
    phase_turns = jnp.mod(freq_x * mult_x + freq_y * mult_y, BOX)
    angles = phase_turns.astype(jnp.float32) * (2.0 * math.pi / BOX)
    return (jnp.cos(angles), jnp.sin(angles))


def pick_rows(bin_index, lookup):
    one_hot = (bin_index[:, None] == jnp.arange(lookup.shape[0], dtype=jnp.int32)[None, :]).astype(
        jnp.float32
    )
    return jnp.dot(
        one_hot, lookup, precision=lax.Precision.HIGHEST, preferred_element_type=jnp.float32
    )


def prepare(particles, weight, ctf_rows, shifts, freq_x, freq_y):
    values = particles.astype(jnp.float32)
    real_part = values[:, 0]
    imag_part = values[:, 1]
    cosine, sine_value = rotation(freq_x[None, :], freq_y[None, :], shifts[:, 0:1], shifts[:, 1:2])
    moved_real = real_part * cosine + imag_part * sine_value
    moved_imag = imag_part * cosine - real_part * sine_value
    factor = weight[None, :] * ctf_rows
    weighted = jnp.stack([factor * moved_real, factor * moved_imag], axis=1).astype(jnp.bfloat16)
    energy = jnp.sum(weight[None, :] * (real_part * real_part + imag_part * imag_part), axis=1)
    return (weighted, energy)


def shifted_tables(projections, freq_x, freq_y):
    offsets = jnp.arange(TSIDE, dtype=jnp.int32) - TSIDE // 2
    mult_x = jnp.repeat(offsets, TSIDE)[:, None]
    mult_y = jnp.tile(offsets, TSIDE)[:, None]
    cosine, sine_value = rotation(freq_x[None, :], freq_y[None, :], mult_x, mult_y)
    cosine = cosine[:, None, :]
    sine_value = sine_value[:, None, :]
    proj_real = projections[:, 0].astype(jnp.float32)[None, :, :]
    proj_imag = projections[:, 1].astype(jnp.float32)[None, :, :]
    moved_real = proj_real * cosine - proj_imag * sine_value
    moved_imag = proj_imag * cosine + proj_real * sine_value
    stacked = jnp.stack([moved_real, moved_imag], axis=2).astype(jnp.bfloat16)
    return stacked.reshape(TSIDE * TSIDE * projections.shape[0], -1)


def slot_scores(slot_rows, bin_index, projections, weight, ctf, freq_x, freq_y):
    orient_count = projections.shape[0]
    lookup = shifted_tables(projections, freq_x, freq_y)
    cross_term = lax.dot_general(
        slot_rows, lookup, (((1,), (1,)), ((), ())), preferred_element_type=jnp.float32
    )
    cross_term = cross_term.reshape(slot_rows.shape[0], TSIDE * TSIDE, orient_count)
    proj_values = projections.astype(jnp.float32)
    magnitude = proj_values[:, 0] * proj_values[:, 0] + proj_values[:, 1] * proj_values[:, 1]
    weighted_ctf = weight[None, :] * ctf * ctf
    power = lax.dot_general(
        weighted_ctf,
        magnitude,
        (((1,), (1,)), ((), ())),
        precision=lax.Precision.HIGHEST,
        preferred_element_type=jnp.float32,
    )
    power_rows = pick_rows(bin_index, power)
    return cross_term - 0.5 * power_rows[:, None, :]


def window(scores, starts, orient_count):
    orient_index = jnp.mod(
        starts[:, None] + jnp.arange(orient_count // 2, dtype=jnp.int32)[None, :], orient_count
    )
    return jnp.take_along_axis(scores, orient_index[:, None, :], axis=2)


def slot_layout(tile_ids, tile_count, capacity):
    positions = jnp.arange(tile_ids.shape[0], dtype=jnp.int32)
    earlier_same = (tile_ids[:, None] == tile_ids[None, :]) & (
        positions[None, :] < positions[:, None]
    )
    slot_rank = jnp.sum(earlier_same.astype(jnp.int32), axis=1)
    slot_index = tile_ids * capacity + slot_rank
    matches = slot_index[None, :] == jnp.arange(tile_count * capacity, dtype=jnp.int32)[:, None]
    slot_owner = jnp.sum(jnp.where(matches, positions[None, :] + 1, 0), axis=1) - 1
    return (slot_index, slot_owner)


def finish(scores, energy_sum):
    scored = scores - 0.5 * energy_sum[:, None, None]
    row_peak = jnp.max(scored, axis=(1, 2))
    log_total = row_peak + jnp.log(jnp.sum(jnp.exp(scored - row_peak[:, None, None]), axis=(1, 2)))
    posterior = jnp.exp(scored - log_total[:, None, None])
    return (posterior, log_total)


def slot_plan(particles, projections, noise_weight, tile_list, ori_start, shifts, defocus_bin):
    tile_count = lax.axis_size("tile")
    band_index = lax.axis_index("shell")
    local_count = particles.shape[0]
    window_count = tile_list.shape[1]
    band_width = particles.shape[2]
    orient_count = projections.shape[0]
    capacity = max(2, (2 * local_count * window_count + tile_count - 1) // tile_count)
    freq_x, freq_y = frequencies(band_index * band_width, band_width)
    ctf = ctf_table(freq_x, freq_y, NBIN)
    weighted, energy = prepare(
        particles, noise_weight, pick_rows(defocus_bin, ctf), shifts, freq_x, freq_y
    )
    weighted = weighted.reshape(local_count, 2 * band_width)
    slot_index, slot_owner = slot_layout(tile_list.reshape(-1), tile_count, capacity)
    occupied = slot_owner >= 0
    item_index = jnp.maximum(slot_owner, 0)
    particle = item_index // window_count
    starts_flat = ori_start.reshape(-1)
    send_rows = jnp.where(
        occupied[:, None], jnp.take(weighted, particle, axis=0), jnp.zeros((), jnp.bfloat16)
    )
    send_rows = send_rows.reshape(tile_count, capacity, 2 * band_width)
    send_labels = jnp.stack(
        [jnp.take(defocus_bin, particle), jnp.take(starts_flat, item_index)], axis=1
    )
    send_labels = send_labels.astype(jnp.bfloat16).reshape(tile_count, capacity, 2)
    payload = lax.all_to_all(send_rows, "tile", split_axis=0, concat_axis=0, tiled=True)
    labels = lax.all_to_all(send_labels, "tile", split_axis=0, concat_axis=0, tiled=True)
    source_count = payload.shape[0]
    slot_count = payload.shape[1]
    slot_rows = payload.reshape(source_count * slot_count, payload.shape[2])
    label_ints = labels.reshape(source_count * slot_count, 2).astype(jnp.int32)
    partial_value = slot_scores(
        slot_rows, label_ints[:, 0], projections, noise_weight, ctf, freq_x, freq_y
    )
    partial_value = partial_value.reshape(
        source_count, slot_count, partial_value.shape[1], partial_value.shape[2]
    )
    returned = lax.all_to_all(partial_value, "tile", split_axis=0, concat_axis=0, tiled=True)
    candidates = returned.shape[2]
    returned = jnp.take(
        returned.reshape(tile_count * capacity, candidates, returned.shape[3]), slot_index, axis=0
    )
    returned = window(returned, starts_flat, orient_count)
    kept = returned.shape[2]
    returned = returned.reshape(local_count, window_count, candidates, kept)
    scores = jnp.transpose(returned, (0, 2, 1, 3)).reshape(
        local_count, candidates, window_count * kept
    )
    scores, energy_sum = lax.psum((scores, energy), "shell")
    return finish(scores, energy_sum)


SHIFT_MAX = 8
HIGH = lax.Precision.HIGHEST


def round_up(value, step):
    return (value + step - 1) // step * step


LANES = 128
MESH = pl.DeviceIdType.MESH


def flip(index, turn, count):
    result = index
    step = 1
    while step < count:
        result = result + step * (turn // step % 2) * (1 - 2 * (index // step % 2))
        step *= 2
    return result


def offset_of(order, fars):
    far = (fars - order // 4) % fars
    return far * 4 + order % 2 * 2 + order % 4 // 2


def place_of(order, fars):
    return order % 4 * fars + (fars - order // 4) % fars


def fused_kernel(
    windows,
    part_ref,
    proj_ref,
    label_ref,
    turn_y_ref,
    turn_x_ref,
    weight_ref,
    ctf_ref,
    ctf_sq_ref,
    cos_ref,
    sin_ref,
    post_ref,
    log_ref,
    part_in,
    proj_in,
    label_in,
    hot,
    wave_y,
    wave_x,
    factor,
    weighted,
    square_sum,
    plain,
    magnitude,
    moved,
    sums,
    core_in,
    side_in,
    far_out,
    far_in,
    pair_out,
    pair_in,
    own_sems,
    send_sems,
    recv_sems,
    back_send,
    back_recv,
):
    tile_count, rows, lines, _ = part_in.shape
    fars = tile_count // 4
    orients = proj_in.shape[1]
    kept = orients // 2
    cands = TSIDE * TSIDE
    middle = cands // 2
    width = weight_ref.shape[1]
    chunks = width // LANES
    band_rows = width // BOX
    count = weighted.shape[0]
    half_windows = windows // 2
    used = cands * half_windows * kept
    me = lax.axis_index("tile")
    band = lax.axis_index("shell")
    other = 1 - band
    core_peer = flip(me, 1, tile_count)
    side_peer = flip(me, 2, tile_count)

    barrier = pltpu.get_barrier_semaphore()
    peers = [(flip(me, offset, tile_count), band) for offset in range(1, tile_count)]
    peers += [(me, other), (side_peer, other)]
    for peer in peers:
        pl.semaphore_signal(barrier, inc=1, device_id=peer, device_id_type=MESH)
    pl.semaphore_wait(barrier, len(peers))

    def remote(source, target, send, recv, peer):
        return pltpu.make_async_remote_copy(
            src_ref=source,
            dst_ref=target,
            send_sem=send,
            recv_sem=recv,
            device_id=peer,
            device_id_type=MESH,
        )

    def piece(ref, tile):
        return ref.at[:, pl.ds(pl.multiple_of(tile * lines, lines), lines), :]

    sent = []
    own_copies = []
    for kind, (source, target) in enumerate(
        ((label_ref, label_in), (part_ref, part_in), (proj_ref, proj_in))
    ):
        if kind:
            copy = pltpu.make_async_copy(piece(source, me), target.at[0], own_sems.at[kind - 1])
            copy.start()
            own_copies.append(copy)
        for order in range(1, tile_count):
            tile = flip(me, offset_of(order, fars), tile_count)
            block = piece(source, tile) if kind else source.at[place_of(order, fars) % fars]
            copy = remote(
                block,
                target.at[order],
                send_sems.at[kind, order],
                recv_sems.at[kind, order],
                (tile, band),
            )
            copy.start()
            sent.append(copy)

    def arrived(kind, target, order):
        remote(
            target.at[order],
            target.at[order],
            send_sems.at[kind, order],
            recv_sems.at[kind, order],
            (core_peer, band),
        ).wait_recv()

    sums[...] = jnp.zeros_like(sums)
    label_in[0] = label_ref[0]
    for order in range(1, tile_count):
        arrived(0, label_in, order)
    groups = []
    for group in range(4):
        total = None
        for order in range(group, tile_count, 4):
            value = label_in[order].astype(jnp.float32)
            total = value if total is None else total + value
        groups.append(total)
    labels = jnp.concatenate(groups, axis=1)
    tiles = [labels[j : j + 1] for j in range(windows)]
    starts = [labels[windows + j : windows + j + 1] for j in range(windows)]
    shift_x = labels[2 * windows : 2 * windows + 1]
    shift_y = labels[2 * windows + 1 : 2 * windows + 2]
    bins = labels[2 * windows + 2 : 2 * windows + 3]

    def one_hot(row, table_rows, base):
        index = lax.broadcasted_iota(jnp.int32, (table_rows, count), 0).astype(jnp.float32)
        return (index == row + base).astype(jnp.float32)

    def pick(one_hots, table):
        return lax.dot_general(
            one_hots,
            table,
            (((0,), (0,)), ((), ())),
            precision=HIGH,
            preferred_element_type=jnp.float32,
        )

    steps = turn_y_ref.shape[0]
    hot[...] = one_hot(bins, NBIN, 0.0)
    wave_y[...] = pick(one_hot(shift_y, steps, float(SHIFT_MAX)), turn_y_ref[...])
    wave_x[...] = pick(one_hot(shift_x, steps, float(SHIFT_MAX)), turn_x_ref[...])
    factor[...] = pick(hot[...], ctf_ref[...])

    def unpack(value):
        plain[...] = value.reshape(rows * lines, LANES).astype(jnp.float32)

    def parts_of(chunk):
        real_part = plain[pl.ds(2 * chunk, rows, stride=lines), :]
        imag_part = plain[pl.ds(2 * chunk + 1, rows, stride=lines), :]
        return real_part, imag_part

    for copy in own_copies:
        copy.wait()

    def weigh(order, carry):
        @pl.when(order > 0)
        def _():
            arrived(1, part_in, order)

        unpack(part_in[order])
        first = pl.multiple_of(place_of(order, fars) * rows, rows)
        span = pl.ds(first, rows)
        energy = jnp.zeros((rows, LANES), jnp.float32)
        for chunk in range(chunks):
            line, side = divmod(chunk, BOX // LANES)
            real_part, imag_part = parts_of(chunk)
            cos_y = wave_y[span, side * LANES : (side + 1) * LANES]
            sin_y = wave_y[span, BOX + side * LANES : BOX + (side + 1) * LANES]
            cos_x = wave_x[span, line : line + 1]
            sin_x = wave_x[span, band_rows + line : band_rows + line + 1]
            cosine = cos_x * cos_y - sin_x * sin_y
            sine_value = sin_x * cos_y + cos_x * sin_y
            columns = slice(chunk * LANES, (chunk + 1) * LANES)
            scale = factor[span, columns]
            weighted[span, columns] = (
                scale * (real_part * cosine + imag_part * sine_value)
            ).astype(jnp.bfloat16)
            weighted[span, width + chunk * LANES : width + (chunk + 1) * LANES] = (
                scale * (imag_part * cosine - real_part * sine_value)
            ).astype(jnp.bfloat16)
            square = real_part * real_part + imag_part * imag_part
            energy += weight_ref[:, columns] * square
        square_sum[span, :] = energy
        return carry

    lax.fori_loop(0, tile_count, weigh, 0)
    energy = lax.dot_general(
        jnp.ones((8, LANES), jnp.float32),
        square_sum[...],
        (((1,), (1,)), ((), ())),
        precision=HIGH,
        preferred_element_type=jnp.float32,
    )
    for half in range(2):
        sums[half, used : used + 8, :] = energy

    def score(order, carry):
        @pl.when(order > 0)
        def _():
            arrived(2, proj_in, order)

        unpack(proj_in[order])
        for chunk in range(chunks):
            columns = slice(chunk * LANES, (chunk + 1) * LANES)
            real_part, imag_part = parts_of(chunk)
            magnitude[:, columns] = real_part * real_part + imag_part * imag_part

            def put(cand, real_value, imag_value):
                span = slice(cand * orients, (cand + 1) * orients)
                moved[span, columns] = real_value.astype(jnp.bfloat16)
                moved[span, width + chunk * LANES : width + (chunk + 1) * LANES] = (
                    imag_value.astype(jnp.bfloat16)
                )

            put(middle, real_part, imag_part)
            for cand in range(middle):
                cosine = cos_ref[cand : cand + 1, columns]
                sine_value = sin_ref[cand : cand + 1, columns]
                real_cos = real_part * cosine
                imag_sin = imag_part * sine_value
                imag_cos = imag_part * cosine
                real_sin = real_part * sine_value
                put(cand, real_cos - imag_sin, imag_cos + real_sin)
                put(cands - 1 - cand, real_cos + imag_sin, imag_cos - real_sin)
        power = lax.dot_general(
            magnitude[...],
            ctf_sq_ref[...],
            (((1,), (1,)), ((), ())),
            precision=HIGH,
            preferred_element_type=jnp.float32,
        )
        half_power = 0.5 * jnp.dot(
            power, hot[...], precision=HIGH, preferred_element_type=jnp.float32
        )
        cross = lax.dot_general(
            moved[...],
            weighted[...],
            (((1,), (1,)), ((), ())),
            preferred_element_type=jnp.float32,
        )
        tile = flip(me, offset_of(order, fars), tile_count).astype(jnp.float32)
        named = [row == tile for row in tiles]
        start = jnp.zeros_like(starts[0])
        for j in range(windows):
            start = jnp.where(named[j], starts[j], start)
        start = start.astype(jnp.int32)
        for cand in range(cands):
            value = cross[cand * orients : (cand + 1) * orients] - half_power
            bit = orients // 2
            while bit:
                turned = pltpu.roll(value, orients - bit, 0)
                value = jnp.where((start & bit) != 0, turned, value)
                bit //= 2
            value = value[:kept]
            for j in range(windows):
                half, place = divmod(j, half_windows)
                first = (cand * half_windows + place) * kept
                span = slice(first, first + kept)
                sums[half, span, :] = jnp.where(named[j], value, sums[half, span, :])
        return carry

    lax.fori_loop(0, tile_count, score, 0)

    near = count // 2
    quarter = count // 4
    copy = remote(
        sums.at[:, :, pl.ds(near, near)],
        core_in,
        back_send.at[0],
        back_recv.at[0],
        (core_peer, band),
    )
    copy.start()
    sent.append(copy)
    copy.wait_recv()
    sums[:, :, :near] = sums[:, :, :near] + core_in[...]

    copies = []
    for way, (half, lane, peer) in enumerate(
        (
            (other, quarter, (side_peer, other)),
            (other, 0, (me, other)),
            (band, quarter, (side_peer, band)),
        )
    ):
        copy = remote(
            sums.at[half, :, pl.ds(lane, quarter)],
            side_in.at[way],
            back_send.at[1 + way],
            back_recv.at[1 + way],
            peer,
        )
        copy.start()
        copies.append(copy)
    total = sums[band, :, :quarter]
    for way, copy in enumerate(copies):
        copy.wait_recv()
        total = total + side_in[way]
    sent += copies
    spare = far_out.shape[1] - total.shape[0]
    total = jnp.concatenate([total, jnp.zeros((spare, quarter), jnp.float32)], axis=0)
    far_out[...] = total.T

    copies = []
    for far in range(1, fars):
        copy = remote(
            far_out.at[pl.ds(far * rows, rows), :],
            far_in.at[far],
            back_send.at[3 + far],
            back_recv.at[3 + far],
            (flip(me, 4 * far, tile_count), band),
        )
        copy.start()
        copies.append(copy)
    total = far_out[:rows, :]
    for far, copy in enumerate(copies):
        copy.wait_recv()
        total = total + far_in[1 + far]
    sent += copies
    pair_out[...] = total
    copy = remote(
        pair_out, pair_in, back_send.at[3 + fars], back_recv.at[3 + fars], (me, other)
    )
    copy.start()
    sent.append(copy)
    inside = lax.broadcasted_iota(jnp.int32, total.shape, 1) < used
    low = jnp.full_like(total, -jnp.inf)
    energy = total[:, used : used + 1]
    own = jnp.where(inside, total, low)
    own_peak = jnp.max(own, axis=1, keepdims=True)
    copy.wait_recv()
    theirs = jnp.where(inside, pair_in[...], low)
    peak = jnp.maximum(own_peak, jnp.max(theirs, axis=1, keepdims=True))
    mass = jnp.sum(jnp.exp(own - peak), axis=1, keepdims=True)
    mass += jnp.sum(jnp.exp(theirs - peak), axis=1, keepdims=True)
    log_total = peak + jnp.log(mass)
    post_ref[band] = jnp.exp(own - log_total)
    post_ref[other] = jnp.exp(theirs - log_total)
    log_ref[...] = jnp.broadcast_to(log_total - 0.5 * energy, log_ref.shape)
    for copy in sent:
        copy.wait_send()


def fused_plan(particles, projections, noise_weight, tile_list, ori_start, shifts, defocus_bin):
    tile_count = lax.axis_size("tile")
    tile_index = lax.axis_index("tile")
    band_index = lax.axis_index("shell")
    local_count, pair, band_width = particles.shape
    orients = projections.shape[0]
    windows = tile_list.shape[1]
    width = band_width // tile_count
    lines = width // BOX
    count = local_count * tile_count
    cands = TSIDE * TSIDE
    fars = tile_count // 4
    half_rows = cands * (windows // 2) * (orients // 2) + 8
    columns = round_up(half_rows, LANES)
    piece = width // LANES * pair

    labels = jnp.concatenate([tile_list, ori_start, shifts, defocus_bin[:, None]], axis=1).T
    labels = labels.astype(jnp.bfloat16)
    label_rows = round_up(labels.shape[0], 16)
    labels = jnp.pad(labels, ((0, label_rows - labels.shape[0]), (0, 0)))
    labels = jnp.stack(
        [
            jnp.pad(labels, ((0, 0), (far * local_count, (fars - 1 - far) * local_count)))
            for far in range(fars)
        ]
    )

    freq_x, freq_y = frequencies(band_index * band_width + tile_index * width, width)
    weight = lax.dynamic_slice_in_dim(noise_weight, tile_index * width, width, 0)
    ctf = ctf_table(freq_x, freq_y, NBIN)
    span = round_up(2 * SHIFT_MAX + 1, 8)
    steps = jnp.arange(span, dtype=jnp.int32) - SHIFT_MAX
    none = jnp.zeros((), jnp.int32)
    own_y = jnp.arange(BOX, dtype=jnp.int32) - BOX // 2
    own_x = freq_x[::BOX]
    turn_y = jnp.concatenate(rotation(own_y[None, :], own_y[None, :], none, steps[:, None]), axis=1)
    turn_x = jnp.concatenate(rotation(own_x[None, :], own_x[None, :], steps[:, None], none), axis=1)
    turn_x = jnp.pad(turn_x, ((0, 0), (0, LANES - 2 * lines)))
    offsets = jnp.arange(TSIDE, dtype=jnp.int32) - TSIDE // 2
    cos_t, sin_t = rotation(
        freq_x[None, :],
        freq_y[None, :],
        jnp.repeat(offsets, TSIDE)[:, None],
        jnp.tile(offsets, TSIDE)[:, None],
    )

    def view(values):
        rows = values.shape[0]
        blocks = values.reshape(rows, pair, band_width // LANES, LANES)
        return jnp.transpose(blocks, (0, 2, 1, 3)).reshape(rows, -1, LANES)

    far_space = pl.BlockSpec(memory_space=pl.ANY)
    near_space = pl.BlockSpec(memory_space=pltpu.VMEM)
    posterior, log_total = pl.pallas_call(
        functools.partial(fused_kernel, windows),
        in_specs=[far_space] * 2 + [near_space] * 8,
        out_specs=[near_space] * 2,
        out_shape=[
            jax.ShapeDtypeStruct((2, local_count, columns), jnp.float32),
            jax.ShapeDtypeStruct((local_count, LANES), jnp.float32),
        ],
        scratch_shapes=[
            pltpu.VMEM((tile_count, local_count, piece, LANES), jnp.bfloat16),
            pltpu.VMEM((tile_count, orients, piece, LANES), jnp.bfloat16),
            pltpu.VMEM((tile_count, label_rows, LANES), jnp.bfloat16),
            pltpu.VMEM((NBIN, count), jnp.float32),
            pltpu.VMEM((count, 2 * BOX), jnp.float32),
            pltpu.VMEM((count, LANES), jnp.float32),
            pltpu.VMEM((count, width), jnp.float32),
            pltpu.VMEM((count, pair * width), jnp.bfloat16),
            pltpu.VMEM((count, LANES), jnp.float32),
            pltpu.VMEM((local_count * piece, LANES), jnp.float32),
            pltpu.VMEM((orients, width), jnp.float32),
            pltpu.VMEM((cands * orients, pair * width), jnp.bfloat16),
            pltpu.VMEM((2, half_rows, count), jnp.float32),
            pltpu.VMEM((2, half_rows, count // 2), jnp.float32),
            pltpu.VMEM((3, half_rows, count // 4), jnp.float32),
            pltpu.VMEM((count // 4, columns), jnp.float32),
            pltpu.VMEM((fars, local_count, columns), jnp.float32),
            pltpu.VMEM((local_count, columns), jnp.float32),
            pltpu.VMEM((local_count, columns), jnp.float32),
            pltpu.SemaphoreType.DMA((2,)),
            pltpu.SemaphoreType.DMA((3, tile_count)),
            pltpu.SemaphoreType.DMA((3, tile_count)),
            pltpu.SemaphoreType.DMA((4 + fars,)),
            pltpu.SemaphoreType.DMA((4 + fars,)),
        ],
        compiler_params=pltpu.CompilerParams(
            collective_id=0, has_side_effects=True, vmem_limit_bytes=56 * 1024 * 1024
        ),
        name="fused",
    )(
        view(particles),
        view(projections),
        labels,
        turn_y,
        turn_x,
        weight[None, :],
        weight[None, :] * ctf,
        weight[None, :] * ctf * ctf,
        cos_t,
        sin_t,
    )
    kept = half_rows - 8
    posterior = posterior[:, :, :kept].reshape(2, local_count, cands, -1)
    posterior = jnp.transpose(posterior, (1, 2, 0, 3)).reshape(local_count, cands, -1)
    return posterior, log_total[:, 0]


def fused_fits(particles, projections, tile_list):
    tile_count = lax.axis_size("tile")
    local_count, _, band_width = particles.shape
    return (
        lax.axis_size("shell") == 2
        and tile_count & (tile_count - 1) == 0
        and tile_count * local_count == 4 * LANES
        and band_width % (BOX * tile_count) == 0
        and projections.shape[0] == local_count
        and tile_list.shape[1] % 2 == 0
    )


def per_device(particles, projections, noise_weight, tile_list, ori_start, shifts, defocus_bin):
    plan = fused_plan if fused_fits(particles, projections, tile_list) else slot_plan
    return plan(
        particles, projections, noise_weight, tile_list, ori_start, shifts, defocus_bin
    )


def solution(mesh):
    in_specs = (
        P("tile", None, "shell"),
        P("tile", None, "shell"),
        P("shell"),
        P("tile", None),
        P("tile", None),
        P("tile", None),
        P("tile"),
    )
    out_specs = (P("tile", None, None), P("tile"))
    return jax.shard_map(
        per_device, mesh=mesh, in_specs=in_specs, out_specs=out_specs, check_vma=False
    )
```

time: 201 us -> 143 us (0.71)
  Pallas kernels: 30.7 us -> 131 us
  blocking collectives: 71.8 us -> 0 us
  waiting for transfers between devices: 54.8 us -> 0 us
  starting transfers between devices: 14.9 us -> 0 us
  local copies, waits for them, and re-layouts: 17.7 us -> 5.2 us
  matrix products: 7.3 us -> 0 us
  other arithmetic: 2.64 us -> 6.33 us
    pallas_call x2 -> x1, Pallas kernels: 30.7 us -> 131 us  [fused_plan(): pl.pallas_call(functools.partial(fused_kernel, windows), in_specs=[far_sp...]
    all_to_all x2 -> x0, waiting for transfers between devices: 54.8 us -> none  [exchange(): lax.all_to_all(blocks, 'tile', split_axis=0, concat_axis=0, tiled=True)]
    all_to_all x1 -> x0, blocking collectives: 42.4 us -> none  [band_plan(): lax.all_to_all(blocks, 'tile', split_axis=0, concat_axis=0, tiled=True)]
    all_gather x2 -> x0, blocking collectives: 29.4 us -> none  [the longest x1 23.5 us: band_plan(): labels = lax.all_gather(labels, 'tile', axis=1, tiled=True)]
    all_to_all x2 -> x0, starting transfers between devices: 14.9 us -> none  [exchange(): lax.all_to_all(blocks, 'tile', split_axis=0, concat_axis=0, tiled=True)]
    reshape x5 -> x1, local copies, waits for them, and re-layouts: 14.4 us -> 0.86 us  [fused_plan(): jnp.transpose(posterior, (1, 2, 0, 3)).reshape(local_count, cands, -1)]
    dot_general x4 -> x0, matrix products: 7.3 us -> none  [the longest x3 5.32 us: pick_rows(): jnp.dot(one_hot, lookup, precision=lax.Precision.HIGHEST, preferred_eleme...]
    another operation x0 -> x4, other arithmetic: none -> 2.66 us
  transfers between devices with their start and end apart: 2 -> 0, of which waited for: 2 -> 0; matrix products, arithmetic and copies ran while one was open for 8% -> 0% of each run, Pallas kernels for 6% -> 0%
where the time goes in v1:
time: 143 us
  Pallas kernels  131 us (92%)
  other arithmetic  6.33 us (4%)
  local copies, waits for them, and re-layouts  5.2 us (4%)
    pallas_call x1, Pallas kernels, fused_plan(): pl.pallas_call(functools.partial(fused_kernel, windows), in_specs=[far_sp...  131 us

profile of v1, /device:TPU:0, one launch (start us, length us, event | category | flops | bytes accessed | tf_op | source)
XLA Modules:
  0.0 143.0 jit_solution(4179088548498784072)
XLA Ops:
  0.7 0.7 convert.15
  1.3 0.7 convert_bitcast_fusion
  2.0 0.7 convert.13
  2.7 0.7 convert.14
  3.4 0.1 mul.237
  3.5 0.1 broadcast_in_dim.9
  3.6 0.1 mul.233
  3.7 0.7 dynamic_slice.3
  4.4 0.0 copy-start
  4.4 0.1 slice.9
  4.5 0.1 fusion.22
  4.6 0.1 copy.21
  4.7 0.6 pad.29.turn_x_ref
  5.3 0.1 pad_bitcast_fusion.3
  5.4 0.6 pad_maximum_fusion.1.label_ref
  6.0 0.2 fusion.11
  6.2 0.6 pad_maximum_fusion.turn_y_ref
  6.8 1.0 fusion.3
  7.8 1.0 fusion.5
  8.8 0.0 copy-done
  8.8 130.7 %fused.1 = (f32[2,32,384]{2,1,0:T(8,128)}, f32[32,128]{1,0:T(8,128)}) custom-call(bf16[32,256,128]{2,1,0:T(8,128)(2,1)} %bitcast.29, bf16[32,256,128]{2,1,0:T(8,128)(2,1)} %bitcast.30, bf16[4,16,128]{2,1,0:T(8,128)(2,1)} %pad_maximum_fusion.1.label_ref, f32[24,512]{1,0:T(8,128)} %pad_maximum_fusion.turn_y_ref, f32[24,128]{1,0:T(8,128)} %pad.29.turn_x_ref, ...), custom_call_target="tpu_custom_call" | custom-call | tf_op jit(solution)/shard_map/fused/pallas_call | solution.py:620
  139.5 1.3 slice_reduce_fusion
  140.9 1.0 copy.22
  141.9 0.2 copy.23
  142.1 0.9 reshape.104
  (11 shorter events, 0.1 us)
Async XLA Ops:
  4.4 4.5 %copy-start = (f32[1024]{0:T(1024)}, f32[1024]{0:T(1024)S(1)}, u32[]{:S(2)}) copy-start(f32[1024]{0:T(1024)S(1)} %dynamic_slice.3) | copy-start | bytes 12292

commit v2 on v1

--- a/solution.py
+++ b/solution.py
@@ -210,29 +210,48 @@
     return result
 
 
+def slot_of(order, fars):
+    late = (order // 4 + fars - 1) // fars
+    rest = late * (order - 4)
+    far = late * (fars - 1 - rest % (fars - 1))
+    near = late * (rest // (fars - 1)) + (1 - late) * order
+    return far, near
+
+
 def offset_of(order, fars):
-    far = (fars - order // 4) % fars
-    return far * 4 + order % 2 * 2 + order % 4 // 2
+    far, near = slot_of(order, fars)
+    return far * 4 + near
 
 
 def place_of(order, fars):
-    return order % 4 * fars + (fars - order // 4) % fars
+    far, near = slot_of(order, fars)
+    return (near % 2 * 2 + near // 2) * fars + far
+
+
+def turn_pair(phase):
+    angle = (phase & (BOX - 1)).astype(jnp.float32) * (2.0 * math.pi / BOX)
+    return jnp.cos(angle), jnp.sin(angle)
 
 
 def fused_kernel(
-    windows,
     part_ref,
     proj_ref,
+    noise_ref,
+    tiles_ref,
+    starts_ref,
+    shifts_ref,
+    bins_ref,
+    post_ref,
+    log_ref,
+    label_row,
     label_ref,
+    weight_ref,
     turn_y_ref,
     turn_x_ref,
-    weight_ref,
     ctf_ref,
     ctf_sq_ref,
     cos_ref,
     sin_ref,
-    post_ref,
-    log_ref,
     part_in,
     proj_in,
     label_in,
@@ -264,8 +283,9 @@
     kept = orients // 2
     cands = TSIDE * TSIDE
     middle = cands // 2
-    width = weight_ref.shape[1]
-    chunks = width // LANES
+    windows = tiles_ref.shape[0]
+    chunks = weight_ref.shape[0]
+    width = chunks * LANES
     band_rows = width // BOX
     count = weighted.shape[0]
     half_windows = windows // 2
@@ -281,6 +301,14 @@
     peers += [(me, other), (side_peer, other)]
     for peer in peers:
         pl.semaphore_signal(barrier, inc=1, device_id=peer, device_id_type=MESH)
+    label_row[...] = jnp.zeros_like(label_row)
+    first = 0
+    for ref in (tiles_ref, starts_ref, shifts_ref, bins_ref):
+        label_row[first : first + ref.shape[0], :rows] = ref[...].astype(jnp.float32)
+        first += ref.shape[0]
+    for far in range(fars):
+        moved_row = pltpu.roll(label_row[...], far * rows, 1) if far else label_row[...]
+        label_ref[far] = moved_row.astype(jnp.bfloat16)
     pl.semaphore_wait(barrier, len(peers))
 
     def remote(source, target, send, recv, peer):
@@ -327,17 +355,73 @@
             (core_peer, band),
         ).wait_recv()
 
+    noise = pltpu.make_async_copy(
+        noise_ref.at[pl.ds(pl.multiple_of(me * chunks, chunks), chunks), :],
+        weight_ref,
+        own_sems.at[2],
+    )
+    noise.start()
+    own_copies.append(noise)
+
     sums[...] = jnp.zeros_like(sums)
+    first_line = (band * tile_count + me) * band_rows
+    steps = turn_y_ref.shape[0]
+    shape = (steps, BOX)
+    step = lax.broadcasted_iota(jnp.int32, shape, 0) - SHIFT_MAX
+    freq = lax.broadcasted_iota(jnp.int32, shape, 1) - BOX // 2
+    cosine, sine_value = turn_pair(step * freq)
+    turn_y_ref[:, :BOX] = cosine
+    turn_y_ref[:, BOX:] = sine_value
+    shape = (steps, LANES)
+    step = lax.broadcasted_iota(jnp.int32, shape, 0) - SHIFT_MAX
+    line = lax.broadcasted_iota(jnp.int32, shape, 1)
+    swap = line >= band_rows
+    cosine, sine_value = turn_pair(step * (first_line + jnp.where(swap, line - band_rows, line)))
+    turn_x_ref[...] = jnp.where(swap, sine_value, cosine)
+    shape = (cos_ref.shape[0], width)
+    cand = lax.broadcasted_iota(jnp.int32, shape, 0)
+    flat = lax.broadcasted_iota(jnp.int32, shape, 1)
+    mult_x = jnp.zeros(shape, jnp.int32)
+    for turn in range(1, TSIDE):
+        mult_x = mult_x + (cand >= turn * TSIDE).astype(jnp.int32)
+    mult_y = cand - TSIDE * mult_x - TSIDE // 2
+    mult_x = mult_x - TSIDE // 2
+    freq_x = first_line + (flat >> (BOX.bit_length() - 1))
+    freq_y = (flat & (BOX - 1)) - BOX // 2
+    cosine, sine_value = turn_pair(freq_x * mult_x + freq_y * mult_y)
+    cos_ref[...] = cosine
+    sin_ref[...] = sine_value
+    for copy in own_copies:
+        copy.wait()
+    shape = (NBIN, LANES)
+    defocus_bin = lax.broadcasted_iota(jnp.int32, shape, 0).astype(jnp.float32)
+    defocus = defocus_base + defocus_step * defocus_bin
+    for chunk in range(chunks):
+        line, side = divmod(chunk, BOX // LANES)
+        lane = lax.broadcasted_iota(jnp.int32, shape, 1) + (side * LANES - BOX // 2)
+        scaled_x = (first_line + line).astype(jnp.float32) / BOX
+        scaled_y = lane.astype(jnp.float32) / BOX
+        radius_sq = scaled_x * scaled_x + scaled_y * scaled_y
+        aberr_phase = (
+            math.pi * wave_length * defocus * radius_sq
+            - 0.5 * math.pi * aberration * wave_length**3 * radius_sq**2
+        )
+        envelope = jnp.exp(-0.25 * b_factor * radius_sq)
+        ctf = -(
+            math.sqrt(1.0 - amplitude**2) * jnp.sin(aberr_phase) + amplitude * jnp.cos(aberr_phase)
+        )
+        ctf = ctf * envelope
+        columns = slice(chunk * LANES, (chunk + 1) * LANES)
+        ctf_ref[:, columns] = weight_ref[chunk : chunk + 1, :] * ctf
+        ctf_sq_ref[:, columns] = weight_ref[chunk : chunk + 1, :] * ctf * ctf
+
     label_in[0] = label_ref[0]
     for order in range(1, tile_count):
         arrived(0, label_in, order)
-    groups = []
-    for group in range(4):
-        total = None
-        for order in range(group, tile_count, 4):
-            value = label_in[order].astype(jnp.float32)
-            total = value if total is None else total + value
-        groups.append(total)
+    groups = [jnp.zeros(label_in.shape[1:], jnp.float32)] * 4
+    for order in range(tile_count):
+        group = place_of(order, fars) // fars
+        groups[group] = groups[group] + label_in[order].astype(jnp.float32)
     labels = jnp.concatenate(groups, axis=1)
     tiles = [labels[j : j + 1] for j in range(windows)]
     starts = [labels[windows + j : windows + j + 1] for j in range(windows)]
@@ -358,7 +442,6 @@
             preferred_element_type=jnp.float32,
         )
 
-    steps = turn_y_ref.shape[0]
     hot[...] = one_hot(bins, NBIN, 0.0)
     wave_y[...] = pick(one_hot(shift_y, steps, float(SHIFT_MAX)), turn_y_ref[...])
     wave_x[...] = pick(one_hot(shift_x, steps, float(SHIFT_MAX)), turn_x_ref[...])
@@ -371,9 +454,6 @@
         real_part = plain[pl.ds(2 * chunk, rows, stride=lines), :]
         imag_part = plain[pl.ds(2 * chunk + 1, rows, stride=lines), :]
         return real_part, imag_part
-
-    for copy in own_copies:
-        copy.wait()
 
     def weigh(order, carry):
         @pl.when(order > 0)
@@ -402,7 +482,7 @@
                 scale * (imag_part * cosine - real_part * sine_value)
             ).astype(jnp.bfloat16)
             square = real_part * real_part + imag_part * imag_part
-            energy += weight_ref[:, columns] * square
+            energy += weight_ref[chunk : chunk + 1, :] * square
         square_sum[span, :] = energy
         return carry
 
@@ -557,22 +637,26 @@
     mass = jnp.sum(jnp.exp(own - peak), axis=1, keepdims=True)
     mass += jnp.sum(jnp.exp(theirs - peak), axis=1, keepdims=True)
     log_total = peak + jnp.log(mass)
-    post_ref[band] = jnp.exp(own - log_total)
-    post_ref[other] = jnp.exp(theirs - log_total)
-    log_ref[...] = jnp.broadcast_to(log_total - 0.5 * energy, log_ref.shape)
+    own = jnp.exp(own - log_total)
+    theirs = jnp.exp(theirs - log_total)
+    low = jnp.where(band == 0, own, theirs)
+    high = jnp.where(band == 0, theirs, own)
+    span = half_windows * kept
+    for cand in range(cands):
+        columns = slice(cand * span, (cand + 1) * span)
+        post_ref[cand] = jnp.concatenate([low[:, columns], high[:, columns]], axis=1)
+    evidence = jnp.broadcast_to(log_total - 0.5 * energy, (rows, LANES))
+    log_ref[...] = evidence.T[:1, :]
     for copy in sent:
         copy.wait_send()
 
 
 def fused_plan(particles, projections, noise_weight, tile_list, ori_start, shifts, defocus_bin):
     tile_count = lax.axis_size("tile")
-    tile_index = lax.axis_index("tile")
-    band_index = lax.axis_index("shell")
     local_count, pair, band_width = particles.shape
     orients = projections.shape[0]
     windows = tile_list.shape[1]
     width = band_width // tile_count
-    lines = width // BOX
     count = local_count * tile_count
     cands = TSIDE * TSIDE
     fars = tile_count // 4
@@ -580,35 +664,9 @@
     columns = round_up(half_rows, LANES)
     piece = width // LANES * pair
 
-    labels = jnp.concatenate([tile_list, ori_start, shifts, defocus_bin[:, None]], axis=1).T
-    labels = labels.astype(jnp.bfloat16)
-    label_rows = round_up(labels.shape[0], 16)
-    labels = jnp.pad(labels, ((0, label_rows - labels.shape[0]), (0, 0)))
-    labels = jnp.stack(
-        [
-            jnp.pad(labels, ((0, 0), (far * local_count, (fars - 1 - far) * local_count)))
-            for far in range(fars)
-        ]
-    )
-
-    freq_x, freq_y = frequencies(band_index * band_width + tile_index * width, width)
-    weight = lax.dynamic_slice_in_dim(noise_weight, tile_index * width, width, 0)
-    ctf = ctf_table(freq_x, freq_y, NBIN)
-    span = round_up(2 * SHIFT_MAX + 1, 8)
-    steps = jnp.arange(span, dtype=jnp.int32) - SHIFT_MAX
-    none = jnp.zeros((), jnp.int32)
-    own_y = jnp.arange(BOX, dtype=jnp.int32) - BOX // 2
-    own_x = freq_x[::BOX]
-    turn_y = jnp.concatenate(rotation(own_y[None, :], own_y[None, :], none, steps[:, None]), axis=1)
-    turn_x = jnp.concatenate(rotation(own_x[None, :], own_x[None, :], steps[:, None], none), axis=1)
-    turn_x = jnp.pad(turn_x, ((0, 0), (0, LANES - 2 * lines)))
-    offsets = jnp.arange(TSIDE, dtype=jnp.int32) - TSIDE // 2
-    cos_t, sin_t = rotation(
-        freq_x[None, :],
-        freq_y[None, :],
-        jnp.repeat(offsets, TSIDE)[:, None],
-        jnp.tile(offsets, TSIDE)[:, None],
-    )
+    label_rows = round_up(2 * windows + shifts.shape[1] + 1, 16)
+    steps = round_up(2 * SHIFT_MAX + 1, 8)
+    half_cands = round_up(cands // 2, 8)
 
     def view(values):
         rows = values.shape[0]
@@ -618,14 +676,23 @@
     far_space = pl.BlockSpec(memory_space=pl.ANY)
     near_space = pl.BlockSpec(memory_space=pltpu.VMEM)
     posterior, log_total = pl.pallas_call(
-        functools.partial(fused_kernel, windows),
-        in_specs=[far_space] * 2 + [near_space] * 8,
+        fused_kernel,
+        in_specs=[far_space] * 3 + [near_space] * 4,
         out_specs=[near_space] * 2,
         out_shape=[
-            jax.ShapeDtypeStruct((2, local_count, columns), jnp.float32),
-            jax.ShapeDtypeStruct((local_count, LANES), jnp.float32),
+            jax.ShapeDtypeStruct((cands, local_count, windows * (orients // 2)), jnp.float32),
+            jax.ShapeDtypeStruct((1, local_count), jnp.float32),
         ],
         scratch_shapes=[
+            pltpu.VMEM((label_rows, LANES), jnp.float32),
+            pltpu.VMEM((fars, label_rows, LANES), jnp.bfloat16),
+            pltpu.VMEM((width // LANES, LANES), jnp.float32),
+            pltpu.VMEM((steps, 2 * BOX), jnp.float32),
+            pltpu.VMEM((steps, LANES), jnp.float32),
+            pltpu.VMEM((NBIN, width), jnp.float32),
+            pltpu.VMEM((NBIN, width), jnp.float32),
+            pltpu.VMEM((half_cands, width), jnp.float32),
+            pltpu.VMEM((half_cands, width), jnp.float32),
             pltpu.VMEM((tile_count, local_count, piece, LANES), jnp.bfloat16),
             pltpu.VMEM((tile_count, orients, piece, LANES), jnp.bfloat16),
             pltpu.VMEM((tile_count, label_rows, LANES), jnp.bfloat16),
@@ -645,7 +712,7 @@
             pltpu.VMEM((fars, local_count, columns), jnp.float32),
             pltpu.VMEM((local_count, columns), jnp.float32),
             pltpu.VMEM((local_count, columns), jnp.float32),
-            pltpu.SemaphoreType.DMA((2,)),
+            pltpu.SemaphoreType.DMA((3,)),
             pltpu.SemaphoreType.DMA((3, tile_count)),
             pltpu.SemaphoreType.DMA((3, tile_count)),
             pltpu.SemaphoreType.DMA((4 + fars,)),
@@ -658,19 +725,13 @@
     )(
         view(particles),
         view(projections),
-        labels,
-        turn_y,
-        turn_x,
-        weight[None, :],
-        weight[None, :] * ctf,
-        weight[None, :] * ctf * ctf,
-        cos_t,
-        sin_t,
-    )
-    kept = half_rows - 8
-    posterior = posterior[:, :, :kept].reshape(2, local_count, cands, -1)
-    posterior = jnp.transpose(posterior, (1, 2, 0, 3)).reshape(local_count, cands, -1)
-    return posterior, log_total[:, 0]
+        noise_weight.reshape(-1, LANES),
+        tile_list.T,
+        ori_start.T,
+        shifts.T,
+        defocus_bin[None, :],
+    )
+    return jnp.transpose(posterior, (1, 0, 2)), log_total[0]
 
 
 def fused_fits(particles, projections, tile_list):

time: 143 us -> 130 us (0.909)
  other arithmetic: 6.33 us -> 0 us
  Pallas kernels: 131 us -> 126 us
  local copies, waits for them, and re-layouts: 5.2 us -> 2.74 us
    pallas_call x1, Pallas kernels: 131 us -> 126 us  [fused_plan(): pl.pallas_call(fused_kernel, in_specs=[far_space] * 3 + [near_space] * 4,...]
    unnamed x2, local copies, waits for them, and re-layouts: 0.01 us -> 2.74 us
    another operation x4 -> x0, other arithmetic: 2.66 us -> none
    slice x3 -> x0, local copies, waits for them, and re-layouts: 2.46 us -> none  [the longest x1 1.34 us: fused_plan(): return (posterior, log_total[:, 0])]
where the time goes in v2:
time: 130 us; the launch traced here: 129 us
  Pallas kernels  126 us (97%)
  local copies, waits for them, and re-layouts  2.74 us (2%)
    pallas_call x1, Pallas kernels, fused_plan(): pl.pallas_call(fused_kernel, in_specs=[far_space] * 3 + [near_space] * 4,...  126 us
    unnamed x2, local copies, waits for them, and re-layouts  2.74 us

profile of v2, /device:TPU:0, one launch (start us, length us, event | category | flops | bytes accessed | tf_op | source)
XLA Modules:
  0.0 129.5 jit_solution(7782887398160579989)
XLA Ops:
  0.6 126.1 %fused.1 = (f32[9,32,64]{2,1,0:T(8,128)}, f32[1,32]{1,0:T(1,128)}) custom-call(bf16[32,256,128]{2,1,0:T(8,128)(2,1)} %bitcast.17, bf16[32,256,128]{2,1,0:T(8,128)(2,1)} %bitcast.18, f32[128,128]{1,0:T(8,128)} %bitcast.20, s32[4,32]{1,0:T(4,128)} %bitcast.21, s32[4,32]{1,0:T(4,128)} %bitcast.22, s32[2,32]{1,0:T(2,128)} %bitcast.23, s32[1,32]{1,0:T(1,128)} %bitcast.24), custom_call_target="tpu_custom_call" | custom-call | tf_op jit(solution)/shard_map/fused/pallas_call | solution.py:678
  126.7 1.6 %copy.13 = f32[32,9,64]{2,0,1:T(8,128)} copy(f32[32,9,64]{2,0,1:T(8,128)} %bitcast.19) | data formatting | bytes 147456
  128.3 1.2 copy.14

commit v3 on v2

--- a/solution.py
+++ b/solution.py
@@ -198,6 +198,7 @@
 
 
 LANES = 128
+CODE_TOP = 32000.0
 MESH = pl.DeviceIdType.MESH
 
 
@@ -241,8 +242,8 @@
     starts_ref,
     shifts_ref,
     bins_ref,
-    post_ref,
-    log_ref,
+    low_ref,
+    high_ref,
     label_row,
     label_ref,
     weight_ref,
@@ -260,13 +261,18 @@
     wave_x,
     factor,
     weighted,
+    local_part,
+    local_noise,
+    noise_rows,
     square_sum,
     plain,
     magnitude,
     moved,
     sums,
     core_in,
+    side_out,
     side_in,
+    far_sum,
     far_out,
     far_in,
     pair_out,
@@ -362,6 +368,12 @@
     )
     noise.start()
     own_copies.append(noise)
+    local_copies = [
+        pltpu.make_async_copy(part_ref, local_part, own_sems.at[3]),
+        pltpu.make_async_copy(noise_ref, local_noise, own_sems.at[4]),
+    ]
+    for copy in local_copies:
+        copy.start()
 
     sums[...] = jnp.zeros_like(sums)
     first_line = (band * tile_count + me) * band_rows
@@ -447,6 +459,23 @@
     wave_x[...] = pick(one_hot(shift_x, steps, float(SHIFT_MAX)), turn_x_ref[...])
     factor[...] = pick(hot[...], ctf_ref[...])
 
+    for copy in local_copies:
+        copy.wait()
+    pairs = local_noise.shape[0]
+    for part in range(2):
+        noise_rows[pl.ds(part, pairs, stride=2), :] = local_noise[...]
+
+    def square(particle, carry):
+        total = jnp.zeros((8, LANES), jnp.float32)
+        for first in range(0, 2 * pairs, 16):
+            value = local_part[particle, first : first + 16, :].astype(jnp.float32)
+            value = value * value * noise_rows[first : first + 16, :]
+            total = total + value[:8] + value[8:]
+        square_sum[pl.ds(particle, 1), :] = jnp.sum(total, axis=0, keepdims=True)
+        return carry
+
+    lax.fori_loop(0, rows, square, 0)
+
     def unpack(value):
         plain[...] = value.reshape(rows * lines, LANES).astype(jnp.float32)
 
@@ -463,7 +492,6 @@
         unpack(part_in[order])
         first = pl.multiple_of(place_of(order, fars) * rows, rows)
         span = pl.ds(first, rows)
-        energy = jnp.zeros((rows, LANES), jnp.float32)
         for chunk in range(chunks):
             line, side = divmod(chunk, BOX // LANES)
             real_part, imag_part = parts_of(chunk)
@@ -481,21 +509,9 @@
             weighted[span, width + chunk * LANES : width + (chunk + 1) * LANES] = (
                 scale * (imag_part * cosine - real_part * sine_value)
             ).astype(jnp.bfloat16)
-            square = real_part * real_part + imag_part * imag_part
-            energy += weight_ref[chunk : chunk + 1, :] * square
-        square_sum[span, :] = energy
         return carry
 
     lax.fori_loop(0, tile_count, weigh, 0)
-    energy = lax.dot_general(
-        jnp.ones((8, LANES), jnp.float32),
-        square_sum[...],
-        (((1,), (1,)), ((), ())),
-        precision=HIGH,
-        preferred_element_type=jnp.float32,
-    )
-    for half in range(2):
-        sums[half, used : used + 8, :] = energy
 
     def score(order, carry):
         @pl.when(order > 0)
@@ -578,6 +594,24 @@
     copy.wait_recv()
     sums[:, :, :near] = sums[:, :, :near] + core_in[...]
 
+    def scale_of(peak):
+        return jnp.ceil(jnp.log2(jnp.maximum(peak, 1e-30)))
+
+    def coded(value, scale):
+        return jnp.round(value * (CODE_TOP * jnp.exp2(-scale))).astype(jnp.int32)
+
+    def plain_of(code, scale):
+        return code.astype(jnp.float32) * (jnp.exp2(scale) / CODE_TOP)
+
+    whole = sums[:, :, :near]
+    peak = jnp.max(jnp.max(jnp.abs(whole), axis=0), axis=0, keepdims=True)
+    scale = scale_of(peak)
+    scale_rows = side_out.shape[1] - used
+    for half in range(2):
+        side_out[half, :used, :] = coded(whole[half], scale).astype(jnp.int16)
+        side_out[half, used:, :] = (
+            jnp.broadcast_to(scale, (scale_rows, near)).astype(jnp.int32).astype(jnp.int16)
+        )
     copies = []
     for way, (half, lane, peer) in enumerate(
         (
@@ -587,7 +621,7 @@
         )
     ):
         copy = remote(
-            sums.at[half, :, pl.ds(lane, quarter)],
+            side_out.at[half, :, pl.ds(lane, quarter)],
             side_in.at[way],
             back_send.at[1 + way],
             back_recv.at[1 + way],
@@ -598,11 +632,17 @@
     total = sums[band, :, :quarter]
     for way, copy in enumerate(copies):
         copy.wait_recv()
-        total = total + side_in[way]
+        code = side_in[way].astype(jnp.int32)
+        total = total + plain_of(code[:used], code[used : used + 1].astype(jnp.float32))
     sent += copies
-    spare = far_out.shape[1] - total.shape[0]
-    total = jnp.concatenate([total, jnp.zeros((spare, quarter), jnp.float32)], axis=0)
-    far_out[...] = total.T
+    columns = far_out.shape[1]
+    total = jnp.concatenate([total, jnp.zeros((columns - used, quarter), jnp.float32)], axis=0)
+    total = total.T
+    far_sum[...] = total
+    scale = scale_of(jnp.max(jnp.abs(total), axis=1, keepdims=True))
+    column = lax.broadcasted_iota(jnp.int32, total.shape, 1)
+    code = coded(total, scale)
+    far_out[...] = jnp.where(column >= used, scale.astype(jnp.int32), code).astype(jnp.int16)
 
     copies = []
     for far in range(1, fars):
@@ -615,40 +655,50 @@
         )
         copy.start()
         copies.append(copy)
-    total = far_out[:rows, :]
+    energy = jnp.sum(square_sum[...], axis=1, keepdims=True)
+    total = far_sum[:rows, :]
     for far, copy in enumerate(copies):
         copy.wait_recv()
-        total = total + far_in[1 + far]
+        code = far_in[1 + far].astype(jnp.int32)
+        total = total + plain_of(code, code[:, used : used + 1].astype(jnp.float32))
     sent += copies
+    column = lax.broadcasted_iota(jnp.int32, total.shape, 1)
+    total = jnp.where(column >= used, energy, total)
     pair_out[...] = total
     copy = remote(
         pair_out, pair_in, back_send.at[3 + fars], back_recv.at[3 + fars], (me, other)
     )
     copy.start()
     sent.append(copy)
-    inside = lax.broadcasted_iota(jnp.int32, total.shape, 1) < used
-    low = jnp.full_like(total, -jnp.inf)
-    energy = total[:, used : used + 1]
-    own = jnp.where(inside, total, low)
-    own_peak = jnp.max(own, axis=1, keepdims=True)
     copy.wait_recv()
-    theirs = jnp.where(inside, pair_in[...], low)
-    peak = jnp.maximum(own_peak, jnp.max(theirs, axis=1, keepdims=True))
-    mass = jnp.sum(jnp.exp(own - peak), axis=1, keepdims=True)
-    mass += jnp.sum(jnp.exp(theirs - peak), axis=1, keepdims=True)
+    theirs = pair_in[...]
+    low_ref[...] = jnp.where(band == 0, total, theirs)
+    high_ref[...] = jnp.where(band == 0, theirs, total)
+    for copy in sent:
+        copy.wait_send()
+
+
+def settle_kernel(low_ref, high_ref, post_ref, log_ref):
+    cands, rows, span = post_ref.shape
+    used = cands * span // 2
+    low = low_ref[...]
+    high = high_ref[...]
+    inside = lax.broadcasted_iota(jnp.int32, low.shape, 1) < used
+    least = jnp.full_like(low, -jnp.inf)
+    energy = low[:, used : used + 1] + high[:, used : used + 1]
+    low = jnp.where(inside, low, least)
+    high = jnp.where(inside, high, least)
+    peak = jnp.max(jnp.maximum(low, high), axis=1, keepdims=True)
+    mass = jnp.sum(jnp.exp(low - peak) + jnp.exp(high - peak), axis=1, keepdims=True)
     log_total = peak + jnp.log(mass)
-    own = jnp.exp(own - log_total)
-    theirs = jnp.exp(theirs - log_total)
-    low = jnp.where(band == 0, own, theirs)
-    high = jnp.where(band == 0, theirs, own)
-    span = half_windows * kept
+    low = jnp.exp(low - log_total)
+    high = jnp.exp(high - log_total)
+    half = span // 2
     for cand in range(cands):
-        columns = slice(cand * span, (cand + 1) * span)
+        columns = slice(cand * half, (cand + 1) * half)
         post_ref[cand] = jnp.concatenate([low[:, columns], high[:, columns]], axis=1)
     evidence = jnp.broadcast_to(log_total - 0.5 * energy, (rows, LANES))
     log_ref[...] = evidence.T[:1, :]
-    for copy in sent:
-        copy.wait_send()
 
 
 def fused_plan(particles, projections, noise_weight, tile_list, ori_start, shifts, defocus_bin):
@@ -660,8 +710,9 @@
     count = local_count * tile_count
     cands = TSIDE * TSIDE
     fars = tile_count // 4
-    half_rows = cands * (windows // 2) * (orients // 2) + 8
-    columns = round_up(half_rows, LANES)
+    half_rows = cands * (windows // 2) * (orients // 2)
+    coded_rows = half_rows + 16
+    columns = round_up(half_rows + 1, LANES)
     piece = width // LANES * pair
 
     label_rows = round_up(2 * windows + shifts.shape[1] + 1, 16)
@@ -675,14 +726,11 @@
 
     far_space = pl.BlockSpec(memory_space=pl.ANY)
     near_space = pl.BlockSpec(memory_space=pltpu.VMEM)
-    posterior, log_total = pl.pallas_call(
+    low, high = pl.pallas_call(
         fused_kernel,
         in_specs=[far_space] * 3 + [near_space] * 4,
         out_specs=[near_space] * 2,
-        out_shape=[
-            jax.ShapeDtypeStruct((cands, local_count, windows * (orients // 2)), jnp.float32),
-            jax.ShapeDtypeStruct((1, local_count), jnp.float32),
-        ],
+        out_shape=[pltpu.VMEM((local_count, columns), jnp.float32)] * 2,
         scratch_shapes=[
             pltpu.VMEM((label_rows, LANES), jnp.float32),
             pltpu.VMEM((fars, label_rows, LANES), jnp.bfloat16),
@@ -701,18 +749,23 @@
             pltpu.VMEM((count, LANES), jnp.float32),
             pltpu.VMEM((count, width), jnp.float32),
             pltpu.VMEM((count, pair * width), jnp.bfloat16),
-            pltpu.VMEM((count, LANES), jnp.float32),
+            pltpu.VMEM((local_count, band_width // LANES * pair, LANES), jnp.bfloat16),
+            pltpu.VMEM((band_width // LANES, LANES), jnp.float32),
+            pltpu.VMEM((band_width // LANES * pair, LANES), jnp.float32),
+            pltpu.VMEM((local_count, LANES), jnp.float32),
             pltpu.VMEM((local_count * piece, LANES), jnp.float32),
             pltpu.VMEM((orients, width), jnp.float32),
             pltpu.VMEM((cands * orients, pair * width), jnp.bfloat16),
             pltpu.VMEM((2, half_rows, count), jnp.float32),
             pltpu.VMEM((2, half_rows, count // 2), jnp.float32),
-            pltpu.VMEM((3, half_rows, count // 4), jnp.float32),
+            pltpu.VMEM((2, coded_rows, count // 2), jnp.int16),
+            pltpu.VMEM((3, coded_rows, count // 4), jnp.int16),
             pltpu.VMEM((count // 4, columns), jnp.float32),
-            pltpu.VMEM((fars, local_count, columns), jnp.float32),
+            pltpu.VMEM((count // 4, columns), jnp.int16),
+            pltpu.VMEM((fars, local_count, columns), jnp.int16),
             pltpu.VMEM((local_count, columns), jnp.float32),
             pltpu.VMEM((local_count, columns), jnp.float32),
-            pltpu.SemaphoreType.DMA((3,)),
+            pltpu.SemaphoreType.DMA((5,)),
             pltpu.SemaphoreType.DMA((3, tile_count)),
             pltpu.SemaphoreType.DMA((3, tile_count)),
             pltpu.SemaphoreType.DMA((4 + fars,)),
@@ -731,6 +784,17 @@
         shifts.T,
         defocus_bin[None, :],
     )
+    posterior, log_total = pl.pallas_call(
+        settle_kernel,
+        in_specs=[near_space] * 2,
+        out_specs=[near_space] * 2,
+        out_shape=[
+            jax.ShapeDtypeStruct((cands, local_count, windows * (orients // 2)), jnp.float32),
+            jax.ShapeDtypeStruct((1, local_count), jnp.float32),
+        ],
+        compiler_params=pltpu.CompilerParams(vmem_limit_bytes=4 * 1024 * 1024),
+        name="settle",
+    )(low, high)
     return jnp.transpose(posterior, (1, 0, 2)), log_total[0]
 
 

time: 130 us -> 123 us (0.946)
  Pallas kernels: 126 us -> 122 us
  local copies, waits for them, and re-layouts: 2.74 us -> 0 us
    pallas_call x1, Pallas kernels: 126 us -> 121 us  [fused_plan(): pl.pallas_call(fused_kernel, in_specs=[far_space] * 3 + [near_space] * 4,...]
    unnamed x2 -> x0, local copies, waits for them, and re-layouts: 2.74 us -> none
where the time goes in v3:
time: 123 us
  Pallas kernels  122 us (99%)
    pallas_call x1, Pallas kernels, fused_plan(): pl.pallas_call(fused_kernel, in_specs=[far_space] * 3 + [near_space] * 4,...  121 us

profile of v3, /device:TPU:0, one launch (start us, length us, event | category | flops | bytes accessed | tf_op | source)
XLA Modules:
  0.0 122.6 jit_solution(4255237102684043144)
XLA Ops:
  0.6 121.0 %fused.1 = (f32[32,384]{1,0:T(8,128)S(1)}, f32[32,384]{1,0:T(8,128)S(1)}) custom-call(bf16[32,256,128]{2,1,0:T(8,128)(2,1)} %bitcast.17, bf16[32,256,128]{2,1,0:T(8,128)(2,1)} %bitcast.18, f32[128,128]{1,0:T(8,128)} %bitcast.19, s32[4,32]{1,0:T(4,128)} %bitcast.20, s32[4,32]{1,0:T(4,128)} %bitcast.21, s32[2,32]{1,0:T(2,128)} %bitcast.22, s32[1,32]{1,0:T(1,128)} %bitcast.23), custom_call_target="tpu_custom_call" | custom-call | tf_op jit(solution)/shard_map/fused/pallas_call | solution.py:729
  121.6 1.0 settle.1

commit v4 on v3

--- a/solution.py
+++ b/solution.py
@@ -232,6 +232,15 @@
 def turn_pair(phase):
     angle = (phase & (BOX - 1)).astype(jnp.float32) * (2.0 * math.pi / BOX)
     return jnp.cos(angle), jnp.sin(angle)
+
+
+def three(value):
+    parts = []
+    for _ in range(3):
+        part = value.astype(jnp.bfloat16)
+        value = value - part.astype(jnp.float32)
+        parts.append(part)
+    return parts
 
 
 def fused_kernel(
@@ -250,13 +259,13 @@
     turn_y_ref,
     turn_x_ref,
     ctf_ref,
-    ctf_sq_ref,
+    power_ref,
     cos_ref,
     sin_ref,
     part_in,
     proj_in,
     label_in,
-    hot,
+    hot_parts,
     wave_y,
     wave_x,
     factor,
@@ -282,6 +291,8 @@
     recv_sems,
     back_send,
     back_recv,
+    core_send,
+    core_recv,
 ):
     tile_count, rows, lines, _ = part_in.shape
     fars = tile_count // 4
@@ -425,7 +436,8 @@
         ctf = ctf * envelope
         columns = slice(chunk * LANES, (chunk + 1) * LANES)
         ctf_ref[:, columns] = weight_ref[chunk : chunk + 1, :] * ctf
-        ctf_sq_ref[:, columns] = weight_ref[chunk : chunk + 1, :] * ctf * ctf
+        for part, value in enumerate(three(0.5 * weight_ref[chunk : chunk + 1, :] * ctf * ctf)):
+            power_ref[part * NBIN : (part + 1) * NBIN, columns] = value
 
     label_in[0] = label_ref[0]
     for order in range(1, tile_count):
@@ -454,10 +466,11 @@
             preferred_element_type=jnp.float32,
         )
 
-    hot[...] = one_hot(bins, NBIN, 0.0)
+    hot = one_hot(bins, NBIN, 0.0)
+    hot_parts[...] = jnp.concatenate([hot] * 3, axis=0).astype(jnp.bfloat16)
     wave_y[...] = pick(one_hot(shift_y, steps, float(SHIFT_MAX)), turn_y_ref[...])
     wave_x[...] = pick(one_hot(shift_x, steps, float(SHIFT_MAX)), turn_x_ref[...])
-    factor[...] = pick(hot[...], ctf_ref[...])
+    factor[...] = pick(hot, ctf_ref[...])
 
     for copy in local_copies:
         copy.wait()
@@ -522,7 +535,8 @@
         for chunk in range(chunks):
             columns = slice(chunk * LANES, (chunk + 1) * LANES)
             real_part, imag_part = parts_of(chunk)
-            magnitude[:, columns] = real_part * real_part + imag_part * imag_part
+            for part, value in enumerate(three(real_part * real_part + imag_part * imag_part)):
+                magnitude[part * orients : (part + 1) * orients, columns] = value
 
             def put(cand, real_value, imag_value):
                 span = slice(cand * orients, (cand + 1) * orients)
@@ -543,13 +557,18 @@
                 put(cands - 1 - cand, real_cos + imag_sin, imag_cos - real_sin)
         power = lax.dot_general(
             magnitude[...],
-            ctf_sq_ref[...],
+            power_ref[...],
             (((1,), (1,)), ((), ())),
-            precision=HIGH,
             preferred_element_type=jnp.float32,
         )
-        half_power = 0.5 * jnp.dot(
-            power, hot[...], precision=HIGH, preferred_element_type=jnp.float32
+        power = power[:orients] + power[orients : 2 * orients] + power[2 * orients :]
+        half_power = jnp.dot(
+            jnp.concatenate(three(power), axis=0),
+            hot_parts[...],
+            preferred_element_type=jnp.float32,
+        )
+        half_power = (
+            half_power[:orients] + half_power[orients : 2 * orients] + half_power[2 * orients :]
         )
         cross = lax.dot_general(
             moved[...],
@@ -582,17 +601,18 @@
 
     near = count // 2
     quarter = count // 4
-    copy = remote(
-        sums.at[:, :, pl.ds(near, near)],
-        core_in,
-        back_send.at[0],
-        back_recv.at[0],
-        (core_peer, band),
-    )
-    copy.start()
-    sent.append(copy)
-    copy.wait_recv()
-    sums[:, :, :near] = sums[:, :, :near] + core_in[...]
+    core_copies = []
+    for turn, half in enumerate((other, band)):
+        copy = remote(
+            sums.at[half, :, pl.ds(near, near)],
+            core_in.at[half],
+            core_send.at[turn],
+            core_recv.at[turn],
+            (core_peer, band),
+        )
+        copy.start()
+        core_copies.append(copy)
+    sent += core_copies
 
     def scale_of(peak):
         return jnp.ceil(jnp.log2(jnp.maximum(peak, 1e-30)))
@@ -603,32 +623,29 @@
     def plain_of(code, scale):
         return code.astype(jnp.float32) * (jnp.exp2(scale) / CODE_TOP)
 
-    whole = sums[:, :, :near]
-    peak = jnp.max(jnp.max(jnp.abs(whole), axis=0), axis=0, keepdims=True)
-    scale = scale_of(peak)
     scale_rows = side_out.shape[1] - used
-    for half in range(2):
-        side_out[half, :used, :] = coded(whole[half], scale).astype(jnp.int16)
+    copies = []
+    for turn, half in enumerate((other, band)):
+        core_copies[turn].wait_recv()
+        whole = sums[half, :, :near] + core_in[half]
+        sums[half, :, :near] = whole
+        scale = scale_of(jnp.max(jnp.abs(whole), axis=0, keepdims=True))
+        side_out[half, :used, :] = coded(whole, scale).astype(jnp.int16)
         side_out[half, used:, :] = (
             jnp.broadcast_to(scale, (scale_rows, near)).astype(jnp.int32).astype(jnp.int16)
         )
-    copies = []
-    for way, (half, lane, peer) in enumerate(
-        (
-            (other, quarter, (side_peer, other)),
-            (other, 0, (me, other)),
-            (band, quarter, (side_peer, band)),
-        )
-    ):
-        copy = remote(
-            side_out.at[half, :, pl.ds(lane, quarter)],
-            side_in.at[way],
-            back_send.at[1 + way],
-            back_recv.at[1 + way],
-            peer,
-        )
-        copy.start()
-        copies.append(copy)
+        ways = ((1, (side_peer, other)), (0, (me, other))) if turn == 0 else ((1, (side_peer, band)),)
+        for lane, peer in ways:
+            way = len(copies)
+            copy = remote(
+                side_out.at[half, :, pl.ds(lane * quarter, quarter)],
+                side_in.at[way],
+                back_send.at[1 + way],
+                back_recv.at[1 + way],
+                peer,
+            )
+            copy.start()
+            copies.append(copy)
     total = sums[band, :, :quarter]
     for way, copy in enumerate(copies):
         copy.wait_recv()
@@ -738,13 +755,13 @@
             pltpu.VMEM((steps, 2 * BOX), jnp.float32),
             pltpu.VMEM((steps, LANES), jnp.float32),
             pltpu.VMEM((NBIN, width), jnp.float32),
-            pltpu.VMEM((NBIN, width), jnp.float32),
+            pltpu.VMEM((3 * NBIN, width), jnp.bfloat16),
             pltpu.VMEM((half_cands, width), jnp.float32),
             pltpu.VMEM((half_cands, width), jnp.float32),
             pltpu.VMEM((tile_count, local_count, piece, LANES), jnp.bfloat16),
             pltpu.VMEM((tile_count, orients, piece, LANES), jnp.bfloat16),
             pltpu.VMEM((tile_count, label_rows, LANES), jnp.bfloat16),
-            pltpu.VMEM((NBIN, count), jnp.float32),
+            pltpu.VMEM((3 * NBIN, count), jnp.bfloat16),
             pltpu.VMEM((count, 2 * BOX), jnp.float32),
             pltpu.VMEM((count, LANES), jnp.float32),
             pltpu.VMEM((count, width), jnp.float32),
@@ -754,7 +771,7 @@
             pltpu.VMEM((band_width // LANES * pair, LANES), jnp.float32),
             pltpu.VMEM((local_count, LANES), jnp.float32),
             pltpu.VMEM((local_count * piece, LANES), jnp.float32),
-            pltpu.VMEM((orients, width), jnp.float32),
+            pltpu.VMEM((3 * orients, width), jnp.bfloat16),
             pltpu.VMEM((cands * orients, pair * width), jnp.bfloat16),
             pltpu.VMEM((2, half_rows, count), jnp.float32),
             pltpu.VMEM((2, half_rows, count // 2), jnp.float32),
@@ -770,6 +787,8 @@
             pltpu.SemaphoreType.DMA((3, tile_count)),
             pltpu.SemaphoreType.DMA((4 + fars,)),
             pltpu.SemaphoreType.DMA((4 + fars,)),
+            pltpu.SemaphoreType.DMA((2,)),
+            pltpu.SemaphoreType.DMA((2,)),
         ],
         compiler_params=pltpu.CompilerParams(
             collective_id=0, has_side_effects=True, vmem_limit_bytes=56 * 1024 * 1024

time: 123 us -> 122 us (level)
  no operation moved by 1% of the time
where the time goes in v4:
time: 122 us
  Pallas kernels  121 us (99%)
    pallas_call x1, Pallas kernels, fused_plan(): pl.pallas_call(fused_kernel, in_specs=[far_space] * 3 + [near_space] * 4,...  120 us

profile of v4, /device:TPU:0, one launch (start us, length us, event | category | flops | bytes accessed | tf_op | source)
XLA Modules:
  0.0 121.7 jit_solution(8043214312452863056)
XLA Ops:
  0.6 120.0 %fused.1 = (f32[32,384]{1,0:T(8,128)S(1)}, f32[32,384]{1,0:T(8,128)S(1)}) custom-call(bf16[32,256,128]{2,1,0:T(8,128)(2,1)} %bitcast.17, bf16[32,256,128]{2,1,0:T(8,128)(2,1)} %bitcast.18, f32[128,128]{1,0:T(8,128)} %bitcast.19, s32[4,32]{1,0:T(4,128)} %bitcast.20, s32[4,32]{1,0:T(4,128)} %bitcast.21, s32[2,32]{1,0:T(2,128)} %bitcast.22, s32[1,32]{1,0:T(1,128)} %bitcast.23), custom_call_target="tpu_custom_call" | custom-call | tf_op jit(solution)/shard_map/fused/pallas_call | solution.py:746
  120.6 1.0 settle.1

commit v5 on v4

--- a/solution.py
+++ b/solution.py
@@ -662,7 +662,7 @@
     far_out[...] = jnp.where(column >= used, scale.astype(jnp.int32), code).astype(jnp.int16)
 
     copies = []
-    for far in range(1, fars):
+    for far in range(fars - 1, 0, -1):
         copy = remote(
             far_out.at[pl.ds(far * rows, rows), :],
             far_in.at[far],
@@ -676,7 +676,7 @@
     total = far_sum[:rows, :]
     for far, copy in enumerate(copies):
         copy.wait_recv()
-        code = far_in[1 + far].astype(jnp.int32)
+        code = far_in[fars - 1 - far].astype(jnp.int32)
         total = total + plain_of(code, code[:, used : used + 1].astype(jnp.float32))
     sent += copies
     column = lax.broadcasted_iota(jnp.int32, total.shape, 1)

time: 122 us -> 121 us (level)
  no operation moved by 1% of the time
where the time goes in v5:
time: 121 us
  Pallas kernels  121 us (100%)
    pallas_call x1, Pallas kernels, fused_plan(): pl.pallas_call(fused_kernel, in_specs=[far_space] * 3 + [near_space] * 4,...  120 us

profile of v5, /device:TPU:0, one launch (start us, length us, event | category | flops | bytes accessed | tf_op | source)
XLA Modules:
  0.0 121.3 jit_solution(16421431805974636622)
XLA Ops:
  0.6 119.6 %fused.1 = (f32[32,384]{1,0:T(8,128)S(1)}, f32[32,384]{1,0:T(8,128)S(1)}) custom-call(bf16[32,256,128]{2,1,0:T(8,128)(2,1)} %bitcast.17, bf16[32,256,128]{2,1,0:T(8,128)(2,1)} %bitcast.18, f32[128,128]{1,0:T(8,128)} %bitcast.19, s32[4,32]{1,0:T(4,128)} %bitcast.20, s32[4,32]{1,0:T(4,128)} %bitcast.21, s32[2,32]{1,0:T(2,128)} %bitcast.22, s32[1,32]{1,0:T(1,128)} %bitcast.23), custom_call_target="tpu_custom_call" | custom-call | tf_op jit(solution)/shard_map/fused/pallas_call | solution.py:746
  120.3 1.0 settle.1
